TPU v7x, 256 devices: a 4x2x16 block of a 4x16x16 slice. The times are simulated.
256 devices in a mesh: grp: 2 (over y), date: 16 (over z), row: 4 (over x), band: 2 (over core).
Axes of the slice: x: 4, y: 2, z: 16, core: 2. Of those that a mesh axis runs over, the one named last changes fastest.
The devices are a block of a 4x16x16 slice.
Arguments:
- reflect: bfloat16 [256, 6, 512, 1024], P('date', 'band', ('grp', 'row')), parts along dimension 2, may hold values from 0 to 0.59765625
- quality: int32 [256, 512, 1024], P('date', ('grp', 'row')), parts along dimension 1, may hold values from 0 to 1073741823
- instrument_ids: int32 [512], P(('grp', 'date')), parts along dimension 0, may hold values from 0 to 2
- day_of_year: int32 [512], P(('grp', 'date')), parts along dimension 0, may hold values from 1 to 365
- image_rank_values: int32 [512], P(('grp', 'date')), parts along dimension 0, may hold values from 0 to 63
- cloud_penalty: int32 [512], P(('grp', 'date')), parts along dimension 0, may hold values from 8 to 32
Outputs:
- composite: bfloat16 [6, 512, 1024], P('band', ('grp', 'row')), parts along dimension 1
- best_date: int32 [512, 1024], P(('grp', 'row')), parts along dimension 0
There are 2 independent parts, one for each index of `grp`. A program takes and returns all parts, laid end to end along the dimension named above; each array names one. Nothing has to cross between parts.
All inputs are finite; a program needn't handle non-finite values.
Results may differ from a plain program's by a relative error of at most 0.001.
Values may be sent and summed in bfloat16 or wider, within the bound.
No kernel may reach another device: no remote copies, remote signals or barrier semaphores. Data moves between devices by JAX's collectives and lax.ppermute only.
A program may use at most 64 MiB of HBM per device.

v0:
```python
import jax
import jax.numpy as jnp
from jax import lax
from jax.sharding import PartitionSpec as P

RADIUS = 4


def with_halo(x, sides, width):
    for axis, dim in sides:
        count, length = (lax.axis_size(axis), x.shape[dim])
        up = [(i, (i + 1) % count) for i in range(count - 1)]
        down = [(j, i) for i, j in up]
        last = lax.slice_in_dim(x, length - width, length, axis=dim)
        leading = lax.slice_in_dim(x, 0, width, axis=dim)
        before = lax.ppermute(last, axis, up)
        after = lax.ppermute(leading, axis, down)
        x = jnp.concatenate([before, x, after], axis=dim)
    return x


def total_of_pieces(x, axis):
    return lax.all_gather(x, axis).max(0)


def split_up(x, dim, count):
    before, after = (x.shape[:dim], x.shape[dim + 1 :])
    return jnp.moveaxis(x.reshape(*before, count, -1, *after), dim, 0)


def sent_and_summed(x, axis, dim):
    parts = split_up(x, dim, lax.axis_size(axis))
    arrived = lax.all_to_all(parts, axis, split_axis=0, concat_axis=0, tiled=True)
    return arrived.astype(jnp.float32).sum(axis=0)


def sent_to_all(x, axis):
    count = lax.axis_size(axis)
    return lax.all_to_all(jnp.broadcast_to(x[None], (count, *x.shape)), axis, 0, 0, tiled=True)


def in_order(parts, dim):
    parts = jnp.moveaxis(parts, 0, dim)
    dims = parts.shape
    return parts.reshape(*dims[:dim], dims[dim] * dims[dim + 1], *dims[dim + 2 :])


def collect(x, axis, dim):
    parts = sent_to_all(x, axis)
    return in_order(parts, dim)


def obstruction(words):
    return (jnp.right_shift(words, 8) & 3) + (jnp.right_shift(words, 10) & 3)


def column_pass(blocked_marker):
    cols = blocked_marker.shape[2]
    widened = jnp.pad(blocked_marker, ((0, 0), (0, 0), (RADIUS, RADIUS)))
    across = jnp.zeros(blocked_marker.shape, jnp.int32)
    for shift in range(-RADIUS, RADIUS + 1):
        across = (
            across
            + (RADIUS + 1 - abs(shift)) * widened[:, :, RADIUS + shift : RADIUS + shift + cols]
        )
    return across


def per_device(reflect, quality, instrument_ids, day_of_year, image_rank_values, cloud_penalty):
    date_dev = quality.shape[0]
    rows_dev = quality.shape[1]
    cols = quality.shape[2]
    ndate = date_dev * lax.axis_size("date")
    own_across = column_pass(obstruction(quality)).astype(jnp.bfloat16)
    across = with_halo(own_across, (("row", 1),), RADIUS).astype(jnp.int32)
    closeness = jnp.zeros((date_dev, rows_dev, cols), jnp.int32)
    for shift in range(-RADIUS, RADIUS + 1):
        closeness = (
            closeness
            + (RADIUS + 1 - abs(shift)) * across[:, RADIUS + shift : RADIUS + shift + rows_dev]
        )
    apart = jnp.abs(day_of_year - 196)
    yearly_cycle_part = jnp.minimum(apart, 365 - apart)
    merit_extra = jnp.where(
        instrument_ids == 1, 300, jnp.where(instrument_ids == 2, 500, 0)
    ).astype(jnp.int32)
    fixed_share_part = 16 * image_rank_values + merit_extra - 4 * yearly_cycle_part
    cell_merit = fixed_share_part[:, None, None] - cloud_penalty[:, None, None] * closeness
    date_ids = lax.axis_index("date") * date_dev + jnp.arange(date_dev, dtype=jnp.int32)
    keys = jnp.max(cell_merit * ndate + date_ids[:, None, None], axis=0)
    top_key = total_of_pieces(keys, "date")
    best = jnp.remainder(top_key, ndate)
    hit = (date_ids[:, None, None] == best[None])[:, None]
    local_vals = jnp.sum(
        jnp.where(hit, reflect, jnp.zeros((), reflect.dtype)), axis=0, dtype=jnp.float32
    )
    part = sent_and_summed(local_vals.astype(jnp.bfloat16), "date", 2).astype(jnp.bfloat16)
    composite = collect(part, "date", 2)
    return (composite, best)


def solution(mesh):
    placed = (
        P("date", "band", ("grp", "row"), None),
        P("date", ("grp", "row"), None),
        P(("grp", "date")),
        P(("grp", "date")),
        P(("grp", "date")),
        P(("grp", "date")),
    )
    return jax.shard_map(
        per_device,
        mesh=mesh,
        in_specs=placed,
        out_specs=(P("band", ("grp", "row"), None), P(("grp", "row"), None)),
        check_vma=False,
    )
```

profile of v0, /device:TPU:38, one launch (start us, length us, event | category | flops | bytes accessed | tf_op | source)
XLA Modules:
  0.0 190.7 jit_solution(5322768957223256278)
XLA Ops:
  7.2 0.1 all-gather.3.cloned.1.call-start
  7.2 2.9 %and_add_fusion = s32[16,64,1024]{2,1,0:T(8,128)S(1)} fusion(s32[16,64,1024]{2,1,0:T(8,128)} %param.7), kind=kLoop, calls=%fused_computation.44 | loop fusion | flops 5242880 | bytes 8388608 | tf_op jit(solution)/shard_map/add | solution.py:54
  10.1 0.0 copy-start.2
  10.1 0.0 copy-start.3
  10.1 0.0 copy-start.4
  10.1 8.8 %fusion.8 = bf16[16,64,1024]{2,1,0:T(8,128)(2,1)S(1)} fusion(s32[16,64,1024]{2,1,0:T(8,128)S(1)} %and_add_fusion), kind=kLoop, calls=%fused_computation.17 | loop fusion | flops 16777216 | bytes 6291456 | tf_op jit(solution)/shard_map/convert_element_type | solution.py:74
  19.0 0.0 copy-start.1
  19.0 0.1 fusion.31
  19.1 1.3 collective-permute-start
  20.4 4.8 %collective-permute-start.1 = (bf16[16,4,1024]{2,1,0:T(4,128)(2,1)S(1)}, bf16[16,4,1024]{2,1,0:T(4,128)(2,1)S(1)}, u32[]{:S(2)}, u32[]{:S(2)}) collective-permute-start(bf16[16,4,1024]{2,1,0:T(4,128)(2,1)S(1)} %get-tuple-element.3), channel_id=1, source_target_pairs={{2,0},{4,2},{6,4},{3,1},{5,3},{7,5},{10,8},{12,10},{14,12},{11,9},... | collective-permute-start | bytes 393224 | tf_op jit(solution)/shard_map/ppermute | solution.py:17
  25.2 0.0 copy-done.2
  25.2 0.0 copy-done.3
  25.2 0.0 copy-done.4
  25.3 1.1 collective-permute-done
  26.3 1.2 collective-permute-done.1
  27.5 1.0 maximum_convert_fusion
  28.5 0.0 copy-done.1
  28.5 5.5 %fusion.19 = s32[64,1024]{1,0:T(8,128)} fusion(s32[16,72,1024]{2,1,0:T(8,128)S(1)} %maximum_convert_fusion, s32[16]{0:T(128)S(1)} %copy-done.1, s32[16]{0:T(128)S(1)} %get-tuple-element.4, s32[16]{0:T(128)S(1)} %get-tuple-element.5), kind=kLoop, calls=%fused_computation.29 | loop fusion | flops 20905984 | bytes 38011072 | tf_op jit(solution)/shard_map/reduce_max | solution.py:90
  34.0 0.1 all-gather.3.cloned.1.call-update
  34.1 91.6 %all-gather.3.cloned.1.call-done = s32[1024,1024]{1,0:T(8,128)} async-done(((s32[64,1024]{1,0:T(8,128)}), s32[1024,1024]{1,0:T(8,128)}) %all-gather.3.cloned.1.call-update) | async-done | bytes 4194320 | tf_op jit(solution)/shard_map/all_gather | solution.py:23
  125.7 2.7 %reduce_max.19 = s32[64,1024]{1,0:T(8,128)S(1)} reduce(s32[16,64,1024]{2,1,0:T(8,128)} %bitcast.5, s32[]{:T(128)} %constant.57.clone.1), dimensions={0}, to_apply=%region_1.2 | reduce | flops 983040 | bytes 4456452 | tf_op jit(solution)/shard_map/reduce_max | solution.py:23
  128.4 0.1 add_select_fusion
  128.5 0.0 copy-start
  128.5 0.6 broadcast_compare_fusion
  129.1 4.6 %select_reduce_fusion = bf16[3,64,1024]{2,1,0:T(8,128)(2,1)S(1)} fusion(bf16[16,3,64,1024]{3,2,1,0:T(8,128)(2,1)} %param.6, pred[16,64,1024]{2,1,0:T(8,128)(4,1)S(1)} %broadcast_compare_fusion), kind=kLoop, calls=%fused_computation | loop fusion | flops 6094848 | bytes 7733248 | tf_op jit(solution)/shard_map/reduce_sum | solution.py:94
  133.7 0.0 copy-done
  133.8 0.5 reshape.31
  134.3 0.2 copy.10
  134.5 0.5 reshape.34
  135.0 23.0 %all_to_all.10 = bf16[16,2,6144]{2,1,0:T(2,128)(2,1)S(1)} all-to-all(bf16[16,2,6144]{2,1,0:T(2,128)(2,1)S(1)} %reshape.34), channel_id=1, replica_groups=mesh['grp'=2,'date'=16,'row'=4,'band'=2] {'date'}, dimensions={0} | all-to-all | bytes 786432 | tf_op jit(solution)/shard_map/all_to_all | solution.py:33
  158.0 0.5 reshape.35
  158.5 0.2 reduce_sum.25
  158.7 0.2 broadcast_in_dim.41
  158.9 0.5 reshape.36
  159.5 22.1 %all_to_all.11 = bf16[16,2,6144]{2,1,0:T(2,128)(2,1)S(1)} all-to-all(bf16[16,2,6144]{2,1,0:T(2,128)(2,1)S(1)} %reshape.36), channel_id=1, replica_groups=mesh['grp'=2,'date'=16,'row'=4,'band'=2] {'date'}, dimensions={0} | all-to-all | bytes 786432 | tf_op jit(solution)/shard_map/all_to_all | solution.py:39
  181.5 0.5 reshape.37
  182.0 0.5 copy.11
  182.5 1.3 reshape.32
  (1 shorter events, 0.0 us)
Async XLA Ops:
  7.2 118.5 %all-gather.3.cloned.1.call-start = ((), (), s32[]{:S(2)}) async-start(), calls=%async_computation.2 | async-start | bytes 4456448 | tf_op jit(solution)/shard_map/all_gather | solution.py:23
  10.1 15.1 %copy-start.2 = (s32[16]{0:T(128)S(1)}, s32[16]{0:T(128)}, u32[]{:S(2)}) copy-start(s32[16]{0:T(128)} %param.8) | copy-start | bytes 196
  10.1 15.1 %copy-start.3 = (s32[16]{0:T(128)S(1)}, s32[16]{0:T(128)}, u32[]{:S(2)}) copy-start(s32[16]{0:T(128)} %param.9) | copy-start | bytes 196
  10.1 15.1 %copy-start.4 = (s32[16]{0:T(128)S(1)}, s32[16]{0:T(128)}, u32[]{:S(2)}) copy-start(s32[16]{0:T(128)} %param.10) | copy-start | bytes 196
  19.0 9.5 %copy-start.1 = (s32[16]{0:T(128)S(1)}, s32[16]{0:T(128)}, u32[]{:S(2)}) copy-start(s32[16]{0:T(128)} %param.11) | copy-start | bytes 196
  19.1 7.2 %collective-permute-start = (bf16[16,4,1024]{2,1,0:T(4,128)(2,1)S(1)}, bf16[16,4,1024]{2,1,0:T(4,128)(2,1)S(1)}, u32[]{:S(2)}, u32[]{:S(2)}) collective-permute-start(bf16[16,4,1024]{2,1,0:T(4,128)(2,1)S(1)} %get-tuple-element.2), channel_id=1, source_target_pairs={{0,2},{2,4},{4,6},{1,3},{3,5},{5,7},{8,10},{10,12},{12,14},{9,11},... | collective-permute-start | bytes 393224 | tf_op jit(solution)/shard_map/ppermute | solution.py:16
  20.4 7.1 %collective-permute-start.1 = (bf16[16,4,1024]{2,1,0:T(4,128)(2,1)S(1)}, bf16[16,4,1024]{2,1,0:T(4,128)(2,1)S(1)}, u32[]{:S(2)}, u32[]{:S(2)}) collective-permute-start(bf16[16,4,1024]{2,1,0:T(4,128)(2,1)S(1)} %get-tuple-element.3), channel_id=1, source_target_pairs={{2,0},{4,2},{6,4},{3,1},{5,3},{7,5},{10,8},{12,10},{14,12},{11,9},... | collective-permute-start | bytes 393224 | tf_op jit(solution)/shard_map/ppermute | solution.py:17
  128.5 5.3 %copy-start = (s32[64,1024]{1,0:T(8,128)}, s32[64,1024]{1,0:T(8,128)S(1)}, u32[]{:S(2)}) copy-start(s32[64,1024]{1,0:T(8,128)S(1)} %add_select_fusion) | copy-start | bytes 786436
Sparse Core Ops, SparseCore 0:
  34.2 91.4 all-gather.2
where the time goes:
time: 193 us; the launch traced here: 191 us
  waiting for transfers between devices  93.9 us (49%)
  blocking collectives  45.1 us (23%)
  other arithmetic  26.4 us (14%)
  between operations  14.3 us (7%)
  starting transfers between devices  6.15 us (3%)
  local copies, waits for them, and re-layouts  4.87 us (3%)
    all_gather x1, waiting for transfers between devices, total_of_pieces(): return lax.all_gather(x, axis).max(0)  91.6 us
    all_to_all x1, blocking collectives, sent_and_summed(): lax.all_to_all(parts, axis, split_axis=0, concat_axis=0, tiled=True)  23 us
    all_to_all x1, blocking collectives, sent_to_all(): lax.all_to_all(jnp.broadcast_to(x[None], (count, *x.shape)), axis, 0, 0,...  22.1 us
    convert_element_type x1, other arithmetic, per_device(): own_across = column_pass(obstruction(quality)).astype(jnp.bfloat16)  8.82 us
    reduce_max x1, other arithmetic, per_device(): keys = jnp.max(cell_merit * ndate + date_ids[:, None, None], axis=0)  5.53 us
    ppermute x1, starting transfers between devices, with_halo(): after = lax.ppermute(leading, axis, down)  4.78 us
    reduce_sum x1, other arithmetic, per_device(): jnp.sum(jnp.where(hit, reflect, jnp.zeros((), reflect.dtype)), axis=0, dt...  4.62 us
  transfers between devices with their start and end apart: 3, of which 3 were waited for; matrix products, arithmetic and copies ran while one was open for 0% of the time, Pallas kernels for 0%

commit v1 on v0

v1 whole, which is shorter than its diff:
```python
import jax
import jax.numpy as jnp
from jax import lax
from jax.experimental import pallas as pl
from jax.experimental.pallas import tpu as pltpu
from jax.sharding import PartitionSpec as P

RADIUS = 4
TILE = 8
GROUP = 4
BLOCK = 256
F32 = jnp.float32
BF16 = jnp.bfloat16
I32 = jnp.int32


def tent(distance):
    return jnp.maximum(RADIUS + 1 - jnp.abs(distance), 0)


def iotas(shape):
    return lax.broadcasted_iota(I32, shape, 0), lax.broadcasted_iota(I32, shape, 1)


def obstruction(words):
    level = ((words >> 8) & 3) + ((words >> 10) & 3)
    return level.astype(F32)


def column_pass(blocked):
    cols = blocked.shape[1]
    side = BLOCK // 2
    k, n = iotas((2 * BLOCK, BLOCK))
    band = tent(k - side - n).astype(F32).astype(BF16)
    out = []
    for start in range(0, cols, BLOCK):
        low = max(0, start - side)
        high = min(cols, start + BLOCK + side)
        first = low - (start - side)
        part = jnp.dot(blocked[:, low:high], band[first : first + high - low], preferred_element_type=F32)
        out.append(part.astype(BF16))
    return jnp.concatenate(out, axis=1)


def terms(ids, days, ranks, penalties, t, dates):
    apart = jnp.abs(days[t] - 196)
    season = jnp.minimum(apart, 365 - apart)
    bonus = jnp.where(ids[t] == 1, 300, jnp.where(ids[t] == 2, 500, 0))
    fixed = 16 * ranks[t] + bonus - 4 * season
    return (fixed * dates + t).astype(F32), (penalties[t] * dates).astype(F32)


def edge_kernel(core, words, out):
    dates = words.shape[0]
    level = obstruction(words[...]).reshape(dates * TILE, -1).astype(BF16)
    row, col = iotas((dates * RADIUS, dates * TILE))
    wanted = (row // RADIUS) * TILE + row % RADIUS + (TILE - RADIUS) * core[0]
    pick = (wanted == col).astype(F32).astype(BF16)
    edge = jnp.dot(pick, level, preferred_element_type=F32).astype(BF16)
    out[...] = column_pass(edge)


def inner_kernel(core, ids, days, ranks, penalties, *refs):
    tiles, (keys, edge) = refs[:-2], refs[-2:]
    step = pl.program_id(0)
    group = tiles[0].shape[0]
    rows = keys.shape[0]
    dates = group * pl.num_programs(0)
    level = jnp.concatenate([obstruction(t[...]).reshape(group * TILE, -1) for t in tiles], axis=0)
    across = column_pass(level.astype(BF16))
    m, k = iotas((group * rows, across.shape[0]))
    same = (m // rows) == (k // TILE) % group
    gap = (k // (group * TILE)) * TILE + k % TILE - TILE * core[0] - m % rows
    mix = jnp.where(same, tent(gap), 0).astype(F32).astype(BF16)
    closeness = jnp.dot(mix, across, preferred_element_type=F32)
    best = None
    for i in range(group):
        own = closeness[i * rows : (i + 1) * rows]
        edge[i] = jnp.where(core[0] == 0, own[:TILE], own[rows - TILE :])
        base, slope = terms(ids, days, ranks, penalties, step * group + i, dates)
        key = base - slope * own
        best = key if best is None else jnp.maximum(best, key)

    @pl.when(step == 0)
    def _():
        keys[...] = best

    @pl.when(step > 0)
    def _():
        keys[...] = jnp.maximum(keys[...], best)


def outer_kernel(place, ids, days, ranks, penalties, keys, edge, halo, out):
    core, own = place[0], place[1]
    dates = edge.shape[0]
    rows = keys.shape[0]
    m, k = iotas((dates * TILE, dates * RADIUS))
    same = (m // TILE) == (k // RADIUS)
    gap = k % RADIUS - m % TILE - RADIUS + (RADIUS + TILE) * core
    mix = jnp.where(same, tent(gap), 0).astype(F32).astype(BF16)
    rest = jnp.dot(mix, halo[...], preferred_element_type=F32)
    best = None
    for t in range(dates):
        base, slope = terms(ids, days, ranks, penalties, t, dates)
        key = base - slope * (edge[t] + rest[t * TILE : (t + 1) * TILE])
        best = key if best is None else jnp.maximum(best, key)
    low_tile, high_tile = (0, rows // TILE - 1)
    across = keys.shape[1] // BLOCK
    ndate = dates * place[2]
    for i in range(rows // TILE):
        key = keys[i * TILE : (i + 1) * TILE]
        if i == low_tile:
            key = jnp.where(core == 0, best, key)
        if i == high_tile:
            key = jnp.where(core == 0, key, best)
        key = key.astype(I32)
        when = key & (dates - 1)
        score = (key - when) // dates
        full = score * ndate + (own * dates + when)
        for j in range(across):
            out[i * across + j] = full[:, j * BLOCK : (j + 1) * BLOCK]


def choose_kernel(keys, reflect, out):
    dates = reflect.shape[0]
    for j in range(keys.shape[1]):
        when = keys[0, j] & (dates - 1)
        hits = [when == t for t in range(1, dates)]
        for k in range(reflect.shape[1]):
            at = (k, slice(None), slice(j * BLOCK, (j + 1) * BLOCK))
            value = reflect[(0, *at)].astype(F32)
            for t in range(1, dates):
                value = jnp.where(hits[t - 1], reflect[(t, *at)].astype(F32), value)
            out[0, j, k, 0] = value.astype(BF16)


def winner_kernel(count, keys, out):
    best = keys[0]
    for s in range(1, keys.shape[0]):
        best = jnp.maximum(best, keys[s])
    out[...] = best & (count[0] - 1)


def merge_kernel(dates, when, values, out):
    sources, bands, halves = values.shape[:3]
    for h in range(halves):
        date = when[h]
        hits = [date >= s * dates[0] for s in range(1, sources)]
        for k in range(bands):
            value = values[0, k, h].astype(F32)
            for s in range(1, sources):
                value = jnp.where(hits[s - 1], values[s, k, h].astype(F32), value)
            out[k, h] = value.astype(BF16)
        out[bands, h] = date.astype(F32).astype(BF16)


def spread_kernel(parts, composite, best):
    sources, groups, halves = parts.shape[:3]
    across = best.shape[1] // BLOCK
    half = best.shape[0] // halves
    for s in range(sources):
        cols = slice((s % across) * BLOCK, (s % across + 1) * BLOCK)
        for h in range(halves):
            top = h * half + (s // across) * TILE
            rows = slice(top, top + TILE)
            for k in range(groups - 1):
                composite[k, rows, cols] = parts[s, k, h]
            best[rows, cols] = parts[s, groups - 1, h].astype(F32).astype(I32)


def per_device(reflect, quality, instrument_ids, day_of_year, image_rank_values, cloud_penalty):
    dates, rows, cols = quality.shape
    bands = reflect.shape[1]
    sources, chips, cores = (lax.axis_size(a) for a in ("date", "row", "band"))
    own, core = lax.axis_index("date"), lax.axis_index("band")
    half = rows // cores
    shape = jax.ShapeDtypeStruct
    smem = pl.BlockSpec(memory_space=pltpu.SMEM)
    vmem = pl.BlockSpec(memory_space=pltpu.VMEM)
    scenes = (instrument_ids, day_of_year, image_rank_values, cloud_penalty)
    core_at = core.astype(I32)[None]

    edge_rows = pl.pallas_call(
        edge_kernel,
        out_shape=shape((dates * RADIUS, cols), BF16),
        grid_spec=pltpu.PrefetchScalarGridSpec(
            num_scalar_prefetch=1,
            grid=(1,),
            in_specs=[pl.BlockSpec((dates, TILE, cols), lambda g, c: (0, c[0] * (rows // TILE - 1), 0))],
            out_specs=pl.BlockSpec((dates * RADIUS, cols), lambda g, c: (0, 0)),
        ),
        name="edge",
    )(core_at, quality)
    links = []
    for x in range(chips - 1):
        links += [(x * cores + 1, (x + 1) * cores), ((x + 1) * cores, x * cores + 1)]
    halo = lax.ppermute(edge_rows, ("row", "band"), links)

    ntile = half // TILE + 1
    inner_keys, edge_part = pl.pallas_call(
        inner_kernel,
        out_shape=(shape((half, cols), F32), shape((dates, TILE, cols), F32)),
        grid_spec=pltpu.PrefetchScalarGridSpec(
            num_scalar_prefetch=5,
            grid=(dates // GROUP,),
            in_specs=[
                pl.BlockSpec((GROUP, TILE, cols), lambda g, c, *_, i=i: (g, c[0] * (ntile - 2) + i, 0)) for i in range(ntile)
            ],
            out_specs=(
                pl.BlockSpec((half, cols), lambda g, *_: (0, 0)),
                pl.BlockSpec((GROUP, TILE, cols), lambda g, *_: (g, 0, 0)),
            ),
        ),
        name="inner",
    )(core_at, *scenes, *([quality] * ntile))

    place = jnp.stack([core, own, jnp.int32(sources)]).astype(I32)
    keys = pl.pallas_call(
        outer_kernel,
        out_shape=shape((sources, TILE, BLOCK), I32),
        in_specs=[smem] * 5 + [vmem] * 3,
        out_specs=vmem,
        name="outer",
    )(place, *scenes, inner_keys, edge_part, halo)

    arrived = lax.all_to_all(keys, "date", 0, 0, tiled=True)
    both = lax.all_gather(keys, "band")

    across = cols // BLOCK
    down = half // TILE
    values = pl.pallas_call(
        choose_kernel,
        out_shape=shape((down, across, bands, cores, TILE, BLOCK), BF16),
        grid=(rows // TILE,),
        in_specs=[
            pl.BlockSpec((1, across, TILE, BLOCK), lambda i: (i // down, i % down, 0, 0)),
            pl.BlockSpec((dates, bands, TILE, cols), lambda i: (0, 0, i, 0)),
        ],
        out_specs=pl.BlockSpec((1, across, bands, 1, TILE, BLOCK), lambda i: (i % down, 0, 0, i // down, 0, 0)),
        name="choose",
    )(both, reflect)
    values = values.reshape(sources, bands * cores * TILE, BLOCK)
    values = lax.all_to_all(values, "date", 0, 0, tiled=True)
    values = values.reshape(sources, bands, cores, TILE, BLOCK)

    won = pl.pallas_call(
        winner_kernel,
        out_shape=shape((TILE, BLOCK), I32),
        in_specs=[smem, vmem],
        out_specs=vmem,
        name="winner",
    )(jnp.full((1,), dates * sources, I32), arrived)
    won = lax.all_gather(won, "band")

    part = pl.pallas_call(
        merge_kernel,
        out_shape=shape((bands + 1, cores, TILE, BLOCK), BF16),
        in_specs=[smem, vmem, vmem],
        out_specs=vmem,
        name="merge",
    )(jnp.full((1,), dates, I32), won, values)
    parts = lax.all_gather(part.reshape((bands + 1) * cores * TILE, BLOCK), "date")
    return pl.pallas_call(
        spread_kernel,
        out_shape=(shape((bands, rows, cols), BF16), shape((rows, cols), I32)),
        in_specs=[vmem],
        out_specs=(vmem, vmem),
        name="spread",
    )(parts.reshape(sources, bands + 1, cores, TILE, BLOCK))


def solution(mesh):
    placed = (
        P("date", "band", ("grp", "row"), None),
        P("date", ("grp", "row"), None),
        P(("grp", "date")),
        P(("grp", "date")),
        P(("grp", "date")),
        P(("grp", "date")),
    )
    return jax.shard_map(
        per_device,
        mesh=mesh,
        in_specs=placed,
        out_specs=(P("band", ("grp", "row"), None), P(("grp", "row"), None)),
        check_vma=False,
    )
```

time: 193 us -> 126 us (0.65)
  waiting for transfers between devices: 93.9 us -> 22.9 us
  starting transfers between devices: 6.15 us -> 35.1 us
  other arithmetic: 26.4 us -> 0.56 us
  Pallas kernels: 0 us -> 21.8 us
  between operations: 14.3 us -> 0.68 us
  local copies, waits for them, and re-layouts: 4.87 us -> 1.4 us
  blocking collectives: 45.1 us -> 41.7 us
    all_gather x1 -> x0, waiting for transfers between devices: 91.6 us -> none  [total_of_pieces(): return lax.all_gather(x, axis).max(0)]
    all_to_all x2 -> x0, blocking collectives: 45.1 us -> none  [the longest x1 23 us: sent_and_summed(): lax.all_to_all(parts, axis, split_axis=0, concat_axis=0, tiled=True)]
    all_gather x0 -> x3, blocking collectives: none -> 41.7 us  [the longest x1 35 us: per_device(): lax.all_gather(part.reshape((bands + 1) * cores * TILE, BLOCK), 'date')]
    all_to_all x0 -> x2, starting transfers between devices: none -> 33 us  [the longest x1 24 us: per_device(): arrived = lax.all_to_all(keys, 'date', 0, 0, tiled=True)]
    all_to_all x0 -> x2, waiting for transfers between devices: none -> 22.9 us  [the longest x1 19.9 us: per_device(): values = lax.all_to_all(values, 'date', 0, 0, tiled=True)]
    pallas_call x0 -> x7, Pallas kernels: none -> 21.8 us  [the longest x1 6.65 us: per_device(): pl.pallas_call(choose_kernel, out_shape=shape((down, across, bands, cores...]
    convert_element_type x2 -> x0, other arithmetic: 9.77 us -> none  [the longest x1 8.82 us: per_device(): own_across = column_pass(obstruction(quality)).astype(jnp.bfloat16)]
    reduce_max x2 -> x0, other arithmetic: 8.2 us -> none  [the longest x1 5.53 us: per_device(): keys = jnp.max(cell_merit * ndate + date_ids[:, None, None], axis=0)]
  transfers between devices with their start and end apart: 3 -> 3, of which waited for: 3 -> 2; matrix products, arithmetic and copies ran while one was open for 0% -> 0% of each run, Pallas kernels for 0% -> 11%
where the time goes in v1:
time: 126 us; the launch traced here: 124 us
  blocking collectives  41.7 us (33%)
  starting transfers between devices  35.1 us (28%)
  waiting for transfers between devices  22.9 us (18%)
  Pallas kernels  21.8 us (17%)
  local copies, waits for them, and re-layouts  1.4 us (1%)
    all_gather x1, blocking collectives, per_device(): lax.all_gather(part.reshape((bands + 1) * cores * TILE, BLOCK), 'date')  35 us
    all_to_all x1, starting transfers between devices, per_device(): arrived = lax.all_to_all(keys, 'date', 0, 0, tiled=True)  24 us
    all_to_all x1, waiting for transfers between devices, per_device(): values = lax.all_to_all(values, 'date', 0, 0, tiled=True)  19.9 us
    all_to_all x1, starting transfers between devices, per_device(): values = lax.all_to_all(values, 'date', 0, 0, tiled=True)  8.98 us
    pallas_call x1, Pallas kernels, per_device(): pl.pallas_call(choose_kernel, out_shape=shape((down, across, bands, cores...  6.65 us
    pallas_call x1, Pallas kernels, per_device(): pl.pallas_call(inner_kernel, out_shape=(shape((half, cols), F32), shape((...  5.75 us
    all_gather x1, blocking collectives, per_device(): both = lax.all_gather(keys, 'band')  3.54 us
    all_gather x1, blocking collectives, per_device(): won = lax.all_gather(won, 'band')  3.13 us
  transfers between devices with their start and end apart: 3, of which 2 were waited for; matrix products, arithmetic and copies ran while one was open for 0% of the time, Pallas kernels for 11%

profile of v1, /device:TPU:38, one launch (start us, length us, event | category | flops | bytes accessed | tf_op | source)
XLA Modules:
  0.0 124.1 jit_solution(2853970898232973022)
XLA Ops:
  0.6 2.2 %edge.1 = bf16[64,1024]{1,0:T(8,128)(2,1)} custom-call(s32[1]{0:T(128)} %bitcast.core, s32[16,64,1024]{2,1,0:T(8,128)} %words.1), custom_call_target="tpu_custom_call" | custom-call | tf_op jit(solution)/shard_map/edge/pallas_call | solution.py:183
  2.8 2.1 %collective-permute-start = (bf16[64,1024]{1,0:T(8,128)(2,1)}, bf16[64,1024]{1,0:T(8,128)(2,1)S(1)}, u32[]{:S(2)}, u32[]{:S(2)}) collective-permute-start(bf16[64,1024]{1,0:T(8,128)(2,1)} %edge.1), channel_id=1, source_target_pairs={{1,2},{2,1},{3,4},{4,3},{5,6},{6,5},{9,10},{10,9},{11,12},{12,11},... | collective-permute-start | bytes 393224 | tf_op jit(solution)/shard_map/ppermute | solution.py:197
  5.0 5.8 %inner.1 = (f32[32,1024]{1,0:T(8,128)}, f32[16,8,1024]{2,1,0:T(8,128)}) custom-call(s32[1]{0:T(128)} %bitcast.core, s32[16]{0:T(128)} %ids.3, s32[16]{0:T(128)} %days.3, s32[16]{0:T(128)} %ranks.3, s32[16]{0:T(128)} %penalties.3, s32[16,64,1024]{2,1,0:T(8,128)} %words.1, s32[16,64,1024]{2,1,0:T(8,128)} %words.1, s32[16,64,1024]{2,1,0:T(8,128)} %words.1, ...), custom_call_target="tpu_custom_call" | custom-call | tf_op jit(solution)/shard_map/inner/pallas_call | solution.py:200
  10.7 0.6 pad_add_fusion.place
  11.3 0.0 collective-permute-done.halo
  11.3 0.0 copy-start.2
  11.3 0.7 copy-done.2
  11.9 2.1 %outer.1 = s32[16,8,256]{2,1,0:T(8,128)} custom-call(s32[3]{0:T(128)} %pad_add_fusion.place, s32[16]{0:T(128)} %ids.3, s32[16]{0:T(128)} %days.3, s32[16]{0:T(128)} %ranks.3, s32[16]{0:T(128)} %penalties.3, f32[32,1024]{1,0:T(8,128)} %get-tuple-element.4.keys, f32[16,8,1024]{2,1,0:T(8,128)} %get-tuple-element.5.edge, bf16[64,1024]{1,0:T(8,128)(2,1)} %copy-done.2), custom_call_target="tpu_custom_call" | custom-call | tf_op jit(solution)/shard_map/outer/pallas_call | solution.py:218
  14.0 24.0 %all-to-all-start = ((s32[16,8,256]{2,1,0:T(8,128)}), s32[16,8,256]{2,1,0:T(8,128)S(1)}, u32[]{:S(2)}, u32[]{:S(2)}) async-start(s32[16,8,256]{2,1,0:T(8,128)} %outer.1), calls=%async_computation | async-start | bytes 262144 | tf_op jit(solution)/shard_map/all_to_all | solution.py:226
  38.0 3.5 %all-gather.1 = s32[32,8,256]{2,1,0:T(8,128)} all-gather(s32[16,8,256]{2,1,0:T(8,128)} %outer.1), channel_id=3, replica_groups=mesh['grp'=2,'date'=16,'row'=4,'band'=2] {'band'}, dimensions={0}, use_global_device_ids=true | all-gather | bytes 393216 | tf_op jit(solution)/shard_map/all_gather | solution.py:227
  41.6 6.6 %choose.1 = bf16[4,4,3,2,8,256]{5,4,3,2,1,0:T(8,128)(2,1)} custom-call(s32[2,16,8,256]{3,2,1,0:T(8,128)} %bitcast.11, bf16[16,3,64,1024]{3,2,1,0:T(8,128)(2,1)} %reflect.1), custom_call_target="tpu_custom_call" | custom-call | tf_op jit(solution)/shard_map/choose/pallas_call | solution.py:231
  48.2 3.0 %all-to-all-done.keys = s32[16,8,256]{2,1,0:T(8,128)S(1)} async-done(((s32[16,8,256]{2,1,0:T(8,128)}), s32[16,8,256]{2,1,0:T(8,128)S(1)}, u32[]{:S(2)}, u32[]{:S(2)}) %all-to-all-start) | async-done | bytes 131104 | tf_op jit(solution)/shard_map/all_to_all | solution.py:226
  51.2 0.0 copy-start.1
  51.2 9.0 %all-to-all-start.1 = ((bf16[16,48,256]{2,1,0:T(8,128)(2,1)}), bf16[16,48,256]{2,1,0:T(8,128)(2,1)S(1)}, u32[]{:S(2)}, u32[]{:S(2)}) async-start(bf16[16,48,256]{2,1,0:T(8,128)(2,1)} %bitcast.10), calls=%async_computation.1 | async-start | bytes 786432 | tf_op jit(solution)/shard_map/all_to_all | solution.py:243
  60.2 0.0 copy-done.1
  60.2 1.5 %winner.1 = s32[8,256]{1,0:T(8,128)} custom-call(s32[1]{0:T(128)} %constant.3.clone.1.count, s32[16,8,256]{2,1,0:T(8,128)} %copy-done.1), custom_call_target="tpu_custom_call" | custom-call | tf_op jit(solution)/shard_map/winner/pallas_call | solution.py:246
  61.8 3.1 %all-gather = s32[16,256]{1,0:T(8,128)} all-gather(s32[8,256]{1,0:T(8,128)} %winner.1), channel_id=2, replica_groups=mesh['grp'=2,'date'=16,'row'=4,'band'=2] {'band'}, dimensions={0}, use_global_device_ids=true | all-gather | bytes 24576 | tf_op jit(solution)/shard_map/all_gather | solution.py:253
  64.9 19.9 %all-to-all-done.1 = bf16[16,48,256]{2,1,0:T(8,128)(2,1)S(1)} async-done(((bf16[16,48,256]{2,1,0:T(8,128)(2,1)}), bf16[16,48,256]{2,1,0:T(8,128)(2,1)S(1)}, u32[]{:S(2)}, u32[]{:S(2)}) %all-to-all-start.1) | async-done | bytes 393248 | tf_op jit(solution)/shard_map/all_to_all | solution.py:243
  84.8 0.0 copy-start
  84.8 0.7 copy-done
  85.5 1.7 %merge.1 = bf16[4,2,8,256]{3,2,1,0:T(8,128)(2,1)} custom-call(s32[1]{0:T(128)} %constant.5.clone.1.dates, s32[2,8,256]{2,1,0:T(8,128)} %bitcast.13, bf16[16,3,2,8,256]{4,3,2,1,0:T(8,128)(2,1)} %bitcast.9), custom_call_target="tpu_custom_call" | custom-call | tf_op jit(solution)/shard_map/merge/pallas_call | solution.py:255
  87.2 35.0 %all_gather.19 = bf16[16,64,256]{2,1,0:T(8,128)(2,1)} all-gather(bf16[1,64,256]{2,1,0:T(8,128)(2,1)} %bitcast.12), channel_id=1, replica_groups=mesh['grp'=2,'date'=16,'row'=4,'band'=2] {'date'}, dimensions={0}, use_global_device_ids=true | all-gather | bytes 557056 | tf_op jit(solution)/shard_map/all_gather | solution.py:262
  122.2 1.9 %spread.1 = (bf16[3,64,1024]{2,1,0:T(8,128)(2,1)}, s32[64,1024]{1,0:T(8,128)}) custom-call(bf16[16,4,2,8,256]{4,3,2,1,0:T(8,128)(2,1)} %bitcast.8), custom_call_target="tpu_custom_call" | custom-call | tf_op jit(solution)/shard_map/spread/pallas_call | solution.py:263
Async XLA Ops:
  2.8 8.5 %collective-permute-start = (bf16[64,1024]{1,0:T(8,128)(2,1)}, bf16[64,1024]{1,0:T(8,128)(2,1)S(1)}, u32[]{:S(2)}, u32[]{:S(2)}) collective-permute-start(bf16[64,1024]{1,0:T(8,128)(2,1)} %edge.1), channel_id=1, source_target_pairs={{1,2},{2,1},{3,4},{4,3},{5,6},{6,5},{9,10},{10,9},{11,12},{12,11},... | collective-permute-start | bytes 393224 | tf_op jit(solution)/shard_map/ppermute | solution.py:197
  11.3 0.7 copy-start.2
  14.0 37.2 %all-to-all-start = ((s32[16,8,256]{2,1,0:T(8,128)}), s32[16,8,256]{2,1,0:T(8,128)S(1)}, u32[]{:S(2)}, u32[]{:S(2)}) async-start(s32[16,8,256]{2,1,0:T(8,128)} %outer.1), calls=%async_computation | async-start | bytes 262144 | tf_op jit(solution)/shard_map/all_to_all | solution.py:226
  51.2 9.0 %copy-start.1 = (s32[16,8,256]{2,1,0:T(8,128)}, s32[16,8,256]{2,1,0:T(8,128)S(1)}, u32[]{:S(2)}) copy-start(s32[16,8,256]{2,1,0:T(8,128)S(1)} %all-to-all-done.keys) | copy-start | bytes 393220
  51.2 33.5 %all-to-all-start.1 = ((bf16[16,48,256]{2,1,0:T(8,128)(2,1)}), bf16[16,48,256]{2,1,0:T(8,128)(2,1)S(1)}, u32[]{:S(2)}, u32[]{:S(2)}) async-start(bf16[16,48,256]{2,1,0:T(8,128)(2,1)} %bitcast.10), calls=%async_computation.1 | async-start | bytes 786432 | tf_op jit(solution)/shard_map/all_to_all | solution.py:243
  84.8 0.7 copy-start

commit v2 on v0

v2 whole, which is shorter than its diff:
```python
import functools

import jax
import jax.numpy as jnp
from jax import lax
from jax.experimental import pallas as pl
from jax.experimental.pallas import tpu as pltpu
from jax.sharding import PartitionSpec as P

RADIUS = 4
TILE = 8
GROUP = 4
BLOCK = 256
FLOOR = 126 * 1024
BIG = 57
F32 = jnp.float32
BF16 = jnp.bfloat16
I32 = jnp.int32


def tent(distance):
    return jnp.maximum(RADIUS + 1 - jnp.abs(distance), 0)


def iotas(shape):
    return lax.broadcasted_iota(I32, shape, 0), lax.broadcasted_iota(I32, shape, 1)


def obstruction(words):
    level = ((words >> 8) & 3) + ((words >> 10) & 3)
    return level.astype(F32)


def column_pass(blocked):
    cols = blocked.shape[1]
    side = BLOCK // 2
    k, n = iotas((2 * BLOCK, BLOCK))
    band = tent(k - side - n).astype(F32).astype(BF16)
    out = []
    for start in range(0, cols, BLOCK):
        low = max(0, start - side)
        high = min(cols, start + BLOCK + side)
        first = low - (start - side)
        part = jnp.dot(blocked[:, low:high], band[first : first + high - low], preferred_element_type=F32)
        out.append(part.astype(BF16))
    return jnp.concatenate(out, axis=1)


def terms(ids, days, ranks, penalties, t, dates):
    apart = jnp.abs(days[t] - 196)
    season = jnp.minimum(apart, 365 - apart)
    bonus = jnp.where(ids[t] == 1, 300, jnp.where(ids[t] == 2, 500, 0))
    fixed = 16 * ranks[t] + bonus - 4 * season
    return (fixed * dates + t).astype(F32), (penalties[t] * dates).astype(F32)


def fetches(source, target, sems, cuts):
    copies = [pltpu.make_async_copy(source.at[src], target.at[dst], sems.at[i]) for i, (src, dst) in enumerate(cuts)]
    for copy in copies:
        copy.start()
    return copies


def edge_kernel(words, first, last, near, sems):
    dates, rows, _ = words.shape
    row, col = iotas((dates * RADIUS, dates * TILE))
    whole = slice(None)
    cuts = [((whole, pl.ds(start, TILE)), side) for side, start in enumerate((0, rows - TILE))]
    copies = fetches(words, near, sems, cuts)
    for side, (out, shift) in enumerate(((first, 0), (last, TILE - RADIUS))):
        wanted = (row // RADIUS) * TILE + row % RADIUS + shift
        pick = (wanted == col).astype(F32).astype(BF16)
        copies[side].wait()
        level = obstruction(near[side]).reshape(dates * TILE, -1).astype(BF16)
        edge = jnp.dot(pick, level, preferred_element_type=F32).astype(BF16)
        out[...] = column_pass(edge)


def inner_kernel(ids, days, ranks, penalties, words, keys, edge, near, sems):
    dates, rows, cols = words.shape
    copies = fetches(words, near, sems, [(pl.ds(t, GROUP), pl.ds(t, GROUP)) for t in range(0, dates, GROUP)])
    m, k = iotas((GROUP * rows, GROUP * rows))
    mix = jnp.where(m // rows == k // rows, tent(k % rows - m % rows), 0).astype(F32).astype(BF16)
    for step, copy in enumerate(copies):
        copy.wait()
        level = obstruction(near[step * GROUP : (step + 1) * GROUP]).reshape(GROUP * rows, cols).astype(BF16)
        across = column_pass(level)
        closeness = jnp.dot(mix, across, preferred_element_type=F32)
        best = None
        for i in range(GROUP):
            t = step * GROUP + i
            own = closeness[i * rows : (i + 1) * rows]
            edge[t, 0] = own[:TILE]
            edge[t, 1] = own[rows - TILE :]
            base, slope = terms(ids, days, ranks, penalties, t, dates)
            key = base - slope * own
            best = key if best is None else jnp.maximum(best, key)
        keys[...] = best if step == 0 else jnp.maximum(keys[...], best)


def small(value):
    return value.astype(F32).astype(BF16)


def coded(number):
    power = jnp.full(number.shape, 2.0**-32, F32)
    for bit in range(6):
        power = power * jnp.where(number & (1 << (7 + bit)) != 0, 2.0 ** (1 << bit), 1.0)
    return (((number & 127) + 128).astype(F32) * power).astype(BF16)


def pick_kernel(ids, days, ranks, penalties, keys, edge, above, below, reflect, out, near, sems):
    dates, bands, rows, cols = reflect.shape
    across = cols // BLOCK
    tall = rows * across // out.shape[0]
    whole = slice(None)
    cuts = [(whole, whole, pl.ds(row, tall)) for row in range(0, rows, tall)]
    copies = fetches(reflect, near, sems, [(cut, cut) for cut in cuts])
    m, k = iotas((dates * TILE, dates * RADIUS))
    same = m // TILE == k // RADIUS
    pairs = [terms(ids, days, ranks, penalties, t, dates) for t in range(dates)]
    ends = []
    for side, halo, shift in ((0, above, -RADIUS), (1, below, TILE)):
        mix = jnp.where(same, tent(k % RADIUS + shift - m % TILE), 0).astype(F32).astype(BF16)
        rest = jnp.dot(mix, halo[...], preferred_element_type=F32)
        best = None
        for t, (base, slope) in enumerate(pairs):
            key = base - slope * (edge[t, side] + rest[t * TILE : (t + 1) * TILE])
            best = key if best is None else jnp.maximum(best, key)
        ends.append(best)
    full = jnp.concatenate([ends[0], keys[TILE : rows - TILE], ends[1]], axis=0).astype(I32)
    full = full + FLOOR * dates
    when = small(full & (dates - 1))
    high = coded(full >> 8)
    low = small(full & 255)
    for i, copy in enumerate(copies):
        copy.wait()
        for j in range(across):
            at = (slice(i * tall, (i + 1) * tall), slice(j * BLOCK, (j + 1) * BLOCK))
            chosen = when[at]
            hits = [chosen == jnp.asarray(t, BF16) for t in range(dates)]
            owner = i * across + j
            for band in range(bands):
                value = near[(0, band, *at)]
                for t in range(1, dates):
                    value = jnp.where(hits[t], near[(t, band, *at)], value)
                out[owner, band * tall : (band + 1) * tall] = value
            out[owner, bands * tall : (bands + 1) * tall] = high[at]
            out[owner, (bands + 1) * tall : (bands + 2) * tall] = low[at]


def scored(low, dates):
    number = low.astype(F32).astype(I32)
    return small(number - (number & (dates - 1)))


def merge_kernel(dates, arrived, out):
    sources, groups, tall, _ = arrived.shape
    bands = groups - 2
    high, low = arrived[0, bands], arrived[0, bands + 1]
    floor = scored(low, dates)
    source = jnp.zeros(high.shape, BF16)
    values = [arrived[0, k] for k in range(bands)]
    for s in range(1, sources):
        h, l = arrived[s, bands], arrived[s, bands + 1]
        better = (h > high) | ((h == high) & (l >= floor))
        high, low = jnp.where(better, h, high), jnp.where(better, l, low)
        floor = jnp.where(better, scored(l, dates), floor)
        source = jnp.where(better, jnp.asarray(s, BF16), source)
        values = [jnp.where(better, arrived[s, k], v) for k, v in enumerate(values)]
    when = low.astype(F32).astype(I32) & (dates - 1)
    date = source.astype(F32) * dates + when.astype(F32)
    parts = [*values, date.astype(BF16)]
    for d in range(sources):
        for k, part in enumerate(parts):
            out[d, k] = part


def spread_kernel(parts, composite, best):
    sources, groups, tall, wide = parts.shape
    across = best.shape[1] // wide
    for s in range(sources):
        rows = slice((s // across) * tall, (s // across + 1) * tall)
        cols = slice((s % across) * wide, (s % across + 1) * wide)
        for k in range(groups - 1):
            composite[k, rows, cols] = parts[s, k]
        best[rows, cols] = parts[s, groups - 1].astype(F32).astype(I32)


def per_device(reflect, quality, instrument_ids, day_of_year, image_rank_values, cloud_penalty):
    dates, rows, cols = quality.shape
    bands = reflect.shape[1]
    sources, chips = lax.axis_size("date"), lax.axis_size("row")
    across = cols // BLOCK
    down = sources // across
    tall = rows // down
    shape = jax.ShapeDtypeStruct
    smem = pl.BlockSpec(memory_space=pltpu.SMEM)
    vmem = pl.BlockSpec(memory_space=pltpu.VMEM)
    hbm = pl.BlockSpec(memory_space=pltpu.HBM)
    scenes = (instrument_ids, day_of_year, image_rank_values, cloud_penalty)

    def grant(mib):
        return pltpu.CompilerParams(vmem_limit_bytes=mib << 20)

    row_shape = shape((dates * RADIUS, cols), BF16)
    first, last = pl.pallas_call(
        edge_kernel,
        out_shape=(row_shape, row_shape),
        in_specs=[hbm],
        out_specs=(vmem, vmem),
        scratch_shapes=[pltpu.VMEM((2, dates, TILE, cols), I32), pltpu.SemaphoreType.DMA((2,))],
        compiler_params=grant(BIG),
        name="edge",
    )(quality)
    onward = [(x, x + 1) for x in range(chips - 1)]
    above = lax.ppermute(last, "row", onward)
    below = lax.ppermute(first, "row", [(j, i) for i, j in onward])

    inner_keys, edge_part = pl.pallas_call(
        inner_kernel,
        out_shape=(shape((rows, cols), F32), shape((dates, 2, TILE, cols), F32)),
        in_specs=[smem] * 4 + [hbm],
        out_specs=(vmem, vmem),
        scratch_shapes=[pltpu.VMEM((dates, rows, cols), I32), pltpu.SemaphoreType.DMA((dates // GROUP,))],
        compiler_params=grant(BIG),
        name="inner",
    )(*scenes, quality)

    packed = pl.pallas_call(
        pick_kernel,
        out_shape=shape((sources, (bands + 2) * tall, BLOCK), BF16),
        in_specs=[smem] * 4 + [vmem] * 4 + [hbm],
        out_specs=vmem,
        scratch_shapes=[pltpu.VMEM((dates, bands, rows, cols), BF16), pltpu.SemaphoreType.DMA((down,))],
        compiler_params=grant(BIG),
        name="pick",
    )(*scenes, inner_keys, edge_part, above, below, reflect)
    arrived = lax.all_to_all(packed, "date", 0, 0, tiled=True)
    part = pl.pallas_call(
        functools.partial(merge_kernel, dates),
        out_shape=shape((sources, bands + 1, tall, BLOCK), BF16),
        in_specs=[vmem],
        out_specs=vmem,
        compiler_params=grant(8),
        name="merge",
    )(arrived.reshape(sources, bands + 2, tall, BLOCK))
    parts = lax.all_to_all(part.reshape(sources, (bands + 1) * tall, BLOCK), "date", 0, 0, tiled=True)
    return pl.pallas_call(
        spread_kernel,
        out_shape=(shape((bands, rows, cols), BF16), shape((rows, cols), I32)),
        in_specs=[vmem],
        out_specs=(vmem, vmem),
        compiler_params=grant(8),
        name="spread",
    )(parts.reshape(sources, bands + 1, tall, BLOCK))


def solution(mesh):
    placed = (
        P("date", "band", ("grp", "row"), None),
        P("date", ("grp", "row"), None),
        P(("grp", "date")),
        P(("grp", "date")),
        P(("grp", "date")),
        P(("grp", "date")),
    )
    return jax.shard_map(
        per_device,
        mesh=mesh,
        in_specs=placed,
        out_specs=(P("band", ("grp", "row"), None), P(("grp", "row"), None)),
        check_vma=False,
    )
```

time: 193 us -> 115 us (0.60); the launches traced: 191 us -> 115 us
  waiting for transfers between devices: 93.9 us -> 0.01 us
  blocking collectives: 45.1 us -> 92.7 us
  other arithmetic: 26.4 us -> 0 us
  Pallas kernels: 0 us -> 14.8 us
  between operations: 14.3 us -> 0.71 us
  local copies, waits for them, and re-layouts: 4.87 us -> 0.67 us
    all_gather x1 -> x0, waiting for transfers between devices: 91.6 us -> none  [total_of_pieces(): return lax.all_gather(x, axis).max(0)]
    all_to_all x2, blocking collectives: 45.1 us -> 92.7 us  [the longest x1 60.1 us: per_device(): arrived = lax.all_to_all(packed, 'date', 0, 0, tiled=True)]
    pallas_call x0 -> x5, Pallas kernels: none -> 14.8 us  [the longest x1 5.74 us: per_device(): pl.pallas_call(inner_kernel, out_shape=(shape((rows, cols), F32), shape((...]
    convert_element_type x2 -> x0, other arithmetic: 9.77 us -> none  [the longest x1 8.82 us: per_device(): own_across = column_pass(obstruction(quality)).astype(jnp.bfloat16)]
    reduce_max x2 -> x0, other arithmetic: 8.2 us -> none  [the longest x1 5.53 us: per_device(): keys = jnp.max(cell_merit * ndate + date_ids[:, None, None], axis=0)]
    reduce_sum x2 -> x0, other arithmetic: 4.79 us -> none  [the longest x1 4.62 us: per_device(): jnp.sum(jnp.where(hit, reflect, jnp.zeros((), reflect.dtype)), axis=0, dt...]
    add x1 -> x0, other arithmetic: 2.87 us -> none  [obstruction(): return (jnp.right_shift(words, 8) & 3) + (jnp.right_shift(words, 10) & 3)]
    ppermute x2, waiting for transfers between devices: 2.28 us -> 0.01 us  [the longest x1 0.01 us: per_device(): below = lax.ppermute(first, 'row', [(j, i) for i, j in onward])]
  transfers between devices with their start and end apart: 3 -> 2, of which waited for: 3 -> 0; matrix products, arithmetic and copies ran while one was open for 0% -> 0% of each run, Pallas kernels for 0% -> 5%
where the time goes in v2:
time: 115 us
  blocking collectives  92.7 us (81%)
  Pallas kernels  14.8 us (13%)
  starting transfers between devices  5.91 us (5%)
    all_to_all x1, blocking collectives, per_device(): arrived = lax.all_to_all(packed, 'date', 0, 0, tiled=True)  60.1 us
    all_to_all x1, blocking collectives, per_device(): lax.all_to_all(part.reshape(sources, (bands + 1) * tall, BLOCK), 'date',...  32.6 us
    pallas_call x1, Pallas kernels, per_device(): pl.pallas_call(inner_kernel, out_shape=(shape((rows, cols), F32), shape((...  5.74 us
    pallas_call x1, Pallas kernels, per_device(): pl.pallas_call(pick_kernel, out_shape=shape((sources, (bands + 2) * tall,...  5.48 us
    ppermute x1, starting transfers between devices, per_device(): below = lax.ppermute(first, 'row', [(j, i) for i, j in onward])  4.6 us
    pallas_call x1, Pallas kernels, per_device(): pl.pallas_call(edge_kernel, out_shape=(row_shape, row_shape), in_specs=[h...  2.59 us
  transfers between devices with their start and end apart: 2, of which 0 were waited for; matrix products, arithmetic and copies ran while one was open for 0% of the time, Pallas kernels for 5%

profile of v2, /device:TPU:38, one launch (start us, length us, event | category | flops | bytes accessed | tf_op | source)
XLA Modules:
  0.0 114.8 jit_solution(5870699909900666352)
XLA Ops:
  0.6 2.6 %edge.1 = (bf16[64,1024]{1,0:T(8,128)(2,1)}, bf16[64,1024]{1,0:T(8,128)(2,1)}) custom-call(s32[16,64,1024]{2,1,0:T(8,128)} %words.3), custom_call_target="tpu_custom_call" | custom-call | tf_op jit(solution)/shard_map/edge/pallas_call | solution.py:207
  3.2 1.3 %collective-permute-start = (bf16[64,1024]{1,0:T(8,128)(2,1)}, bf16[64,1024]{1,0:T(8,128)(2,1)S(1)}, u32[]{:S(2)}, u32[]{:S(2)}) collective-permute-start(bf16[64,1024]{1,0:T(8,128)(2,1)} %get-tuple-element.8), channel_id=1, source_target_pairs={{0,2},{2,4},{4,6},{1,3},{3,5},{5,7},{8,10},{10,12},{12,14},{9,11},... | collective-permute-start | bytes 393224 | tf_op jit(solution)/shard_map/ppermute | solution.py:217
  4.5 4.6 %collective-permute-start.1 = (bf16[64,1024]{1,0:T(8,128)(2,1)}, bf16[64,1024]{1,0:T(8,128)(2,1)S(1)}, u32[]{:S(2)}, u32[]{:S(2)}) collective-permute-start(bf16[64,1024]{1,0:T(8,128)(2,1)} %get-tuple-element.9), channel_id=1, source_target_pairs={{2,0},{4,2},{6,4},{3,1},{5,3},{7,5},{10,8},{12,10},{14,12},{11,9},... | collective-permute-start | bytes 393224 | tf_op jit(solution)/shard_map/ppermute | solution.py:218
  9.1 5.7 %inner.1 = (f32[64,1024]{1,0:T(8,128)}, f32[16,2,8,1024]{3,2,1,0:T(8,128)}) custom-call(s32[16]{0:T(128)} %ids.3, s32[16]{0:T(128)} %days.3, s32[16]{0:T(128)} %ranks.3, s32[16]{0:T(128)} %penalties.3, s32[16,64,1024]{2,1,0:T(8,128)} %words.3), custom_call_target="tpu_custom_call" | custom-call | tf_op jit(solution)/shard_map/inner/pallas_call | solution.py:220
  14.9 0.0 collective-permute-done.above
  14.9 0.0 copy-start
  14.9 0.0 collective-permute-done.1.below
  14.9 0.0 copy-start.1
  14.9 0.6 copy-done
  15.6 0.1 copy-done.1
  15.6 5.5 %pick.1 = bf16[16,80,256]{2,1,0:T(8,128)(2,1)} custom-call(s32[16]{0:T(128)} %ids.3, s32[16]{0:T(128)} %days.3, s32[16]{0:T(128)} %ranks.3, s32[16]{0:T(128)} %penalties.3, f32[64,1024]{1,0:T(8,128)} %get-tuple-element.6.keys, f32[16,2,8,1024]{3,2,1,0:T(8,128)} %get-tuple-element.7.edge, bf16[64,1024]{1,0:T(8,128)(2,1)} %copy-done, ...), custom_call_target="tpu_custom_call" | custom-call | tf_op jit(solution)/shard_map/pick/pallas_call | solution.py:230
  21.1 60.1 %all_to_all.10 = bf16[16,80,256]{2,1,0:T(8,128)(2,1)S(1)} all-to-all(bf16[16,80,256]{2,1,0:T(8,128)(2,1)} %pick.1), channel_id=1, replica_groups=mesh['grp'=2,'date'=16,'row'=4,'band'=2] {'date'}, dimensions={0} | all-to-all | bytes 1310720 | tf_op jit(solution)/shard_map/all_to_all | solution.py:239
  81.2 0.1 merge.1
  81.3 32.6 %all_to_all.11 = bf16[16,64,256]{2,1,0:T(8,128)(2,1)S(1)} all-to-all(bf16[16,64,256]{2,1,0:T(8,128)(2,1)S(1)} %bitcast.5), channel_id=1, replica_groups=mesh['grp'=2,'date'=16,'row'=4,'band'=2] {'date'}, dimensions={0} | all-to-all | bytes 1048576 | tf_op jit(solution)/shard_map/all_to_all | solution.py:248
  113.9 0.9 spread.1
Async XLA Ops:
  3.2 11.7 %collective-permute-start = (bf16[64,1024]{1,0:T(8,128)(2,1)}, bf16[64,1024]{1,0:T(8,128)(2,1)S(1)}, u32[]{:S(2)}, u32[]{:S(2)}) collective-permute-start(bf16[64,1024]{1,0:T(8,128)(2,1)} %get-tuple-element.8), channel_id=1, source_target_pairs={{0,2},{2,4},{4,6},{1,3},{3,5},{5,7},{8,10},{10,12},{12,14},{9,11},... | collective-permute-start | bytes 393224 | tf_op jit(solution)/shard_map/ppermute | solution.py:217
  4.5 10.4 %collective-permute-start.1 = (bf16[64,1024]{1,0:T(8,128)(2,1)}, bf16[64,1024]{1,0:T(8,128)(2,1)S(1)}, u32[]{:S(2)}, u32[]{:S(2)}) collective-permute-start(bf16[64,1024]{1,0:T(8,128)(2,1)} %get-tuple-element.9), channel_id=1, source_target_pairs={{2,0},{4,2},{6,4},{3,1},{5,3},{7,5},{10,8},{12,10},{14,12},{11,9},... | collective-permute-start | bytes 393224 | tf_op jit(solution)/shard_map/ppermute | solution.py:218
  14.9 0.6 copy-start
  14.9 0.7 copy-start.1

commit v3 on v2

--- a/solution.py
+++ b/solution.py
@@ -12,7 +12,7 @@
 GROUP = 4
 BLOCK = 256
 FLOOR = 126 * 1024
-BIG = 57
+BIG = 50
 F32 = jnp.float32
 BF16 = jnp.bfloat16
 I32 = jnp.int32
@@ -46,12 +46,13 @@
     return jnp.concatenate(out, axis=1)
 
 
-def terms(ids, days, ranks, penalties, t, dates):
-    apart = jnp.abs(days[t] - 196)
+def terms(ids, days, ranks, penalties):
+    dates = ids.shape[0]
+    apart = jnp.abs(days - 196)
     season = jnp.minimum(apart, 365 - apart)
-    bonus = jnp.where(ids[t] == 1, 300, jnp.where(ids[t] == 2, 500, 0))
-    fixed = 16 * ranks[t] + bonus - 4 * season
-    return (fixed * dates + t).astype(F32), (penalties[t] * dates).astype(F32)
+    bonus = jnp.where(ids == 1, 300, jnp.where(ids == 2, 500, 0))
+    fixed = (16 * ranks + bonus - 4 * season) * dates + jnp.arange(dates, dtype=I32)
+    return jnp.concatenate([fixed, penalties * dates]).astype(F32)
 
 
 def fetches(source, target, sems, cuts):
@@ -76,7 +77,7 @@
         out[...] = column_pass(edge)
 
 
-def inner_kernel(ids, days, ranks, penalties, words, keys, edge, near, sems):
+def inner_kernel(scenes, words, keys, edge, near, sems):
     dates, rows, cols = words.shape
     copies = fetches(words, near, sems, [(pl.ds(t, GROUP), pl.ds(t, GROUP)) for t in range(0, dates, GROUP)])
     m, k = iotas((GROUP * rows, GROUP * rows))
@@ -92,7 +93,7 @@
             own = closeness[i * rows : (i + 1) * rows]
             edge[t, 0] = own[:TILE]
             edge[t, 1] = own[rows - TILE :]
-            base, slope = terms(ids, days, ranks, penalties, t, dates)
+            base, slope = scenes[t], scenes[dates + t]
             key = base - slope * own
             best = key if best is None else jnp.maximum(best, key)
         keys[...] = best if step == 0 else jnp.maximum(keys[...], best)
@@ -103,22 +104,23 @@
 
 
 def coded(number):
-    power = jnp.full(number.shape, 2.0**-32, F32)
-    for bit in range(6):
+    power = jnp.full(number.shape, 2.0**-64, F32)
+    for bit in range(7):
         power = power * jnp.where(number & (1 << (7 + bit)) != 0, 2.0 ** (1 << bit), 1.0)
     return (((number & 127) + 128).astype(F32) * power).astype(BF16)
 
 
-def pick_kernel(ids, days, ranks, penalties, keys, edge, above, below, reflect, out, near, sems):
+def pick_kernel(own, scenes, keys, edge, above, below, reflect, keep, send, near, when, high, low, sems):
     dates, bands, rows, cols = reflect.shape
     across = cols // BLOCK
-    tall = rows * across // out.shape[0]
+    tall = when.shape[0] * across // (2 * keep.shape[0])
     whole = slice(None)
     cuts = [(whole, whole, pl.ds(row, tall)) for row in range(0, rows, tall)]
     copies = fetches(reflect, near, sems, [(cut, cut) for cut in cuts])
+    parity = own[0] & 1
     m, k = iotas((dates * TILE, dates * RADIUS))
     same = m // TILE == k // RADIUS
-    pairs = [terms(ids, days, ranks, penalties, t, dates) for t in range(dates)]
+    pairs = [(scenes[t], scenes[dates + t]) for t in range(dates)]
     ends = []
     for side, halo, shift in ((0, above, -RADIUS), (1, below, TILE)):
         mix = jnp.where(same, tent(k % RADIUS + shift - m % TILE), 0).astype(F32).astype(BF16)
@@ -130,23 +132,38 @@
         ends.append(best)
     full = jnp.concatenate([ends[0], keys[TILE : rows - TILE], ends[1]], axis=0).astype(I32)
     full = full + FLOOR * dates
-    when = small(full & (dates - 1))
-    high = coded(full >> 8)
-    low = small(full & 255)
+    date = full & (dates - 1)
+    score = (full - date) // dates
+    when[...] = small(date)
+    high[...] = coded(score >> 3)
+    low[...] = small((score & 7) * (2 * dates) + (parity * dates + date))
     for i, copy in enumerate(copies):
         copy.wait()
-        for j in range(across):
-            at = (slice(i * tall, (i + 1) * tall), slice(j * BLOCK, (j + 1) * BLOCK))
-            chosen = when[at]
-            hits = [chosen == jnp.asarray(t, BF16) for t in range(dates)]
-            owner = i * across + j
-            for band in range(bands):
-                value = near[(0, band, *at)]
-                for t in range(1, dates):
-                    value = jnp.where(hits[t], near[(t, band, *at)], value)
-                out[owner, band * tall : (band + 1) * tall] = value
-            out[owner, bands * tall : (bands + 1) * tall] = high[at]
-            out[owner, (bands + 1) * tall : (bands + 2) * tall] = low[at]
+        for j in range(across // 2):
+            slot = i * (across // 2) + j
+            for side, out in enumerate((keep, send)):
+                col = pl.multiple_of((2 * j + (parity ^ side)) * BLOCK, BLOCK)
+                at = (pl.ds(i * tall, tall), pl.ds(col, BLOCK))
+                chosen = when[at]
+                hits = [chosen == jnp.asarray(t, BF16) for t in range(dates)]
+                for band in range(bands):
+                    value = near[(0, band, *at)]
+                    for t in range(1, dates):
+                        value = jnp.where(hits[t], near[(t, band, *at)], value)
+                    out[slot, band] = value
+                out[slot, bands] = high[at]
+                out[slot, bands + 1] = low[at]
+
+
+def pair_kernel(mine, other, out):
+    slots, groups = mine.shape[:2]
+    bands = groups - 2
+    for s in range(slots):
+        high, low = mine[s, bands], mine[s, bands + 1]
+        h, l = other[s, bands], other[s, bands + 1]
+        better = (h > high) | ((h == high) & (l > low))
+        for k in range(groups):
+            out[s, k] = jnp.where(better, other[s, k], mine[s, k])
 
 
 def scored(low, dates):
@@ -155,7 +172,7 @@
 
 
 def merge_kernel(dates, arrived, out):
-    sources, groups, tall, _ = arrived.shape
+    sources, groups = arrived.shape[:2]
     bands = groups - 2
     high, low = arrived[0, bands], arrived[0, bands + 1]
     floor = scored(low, dates)
@@ -176,21 +193,27 @@
             out[d, k] = part
 
 
-def spread_kernel(parts, composite, best):
-    sources, groups, tall, wide = parts.shape
+def spread_kernel(own, mine, other, composite, best):
+    slots, groups, tall, wide = mine.shape
     across = best.shape[1] // wide
-    for s in range(sources):
-        rows = slice((s // across) * tall, (s // across + 1) * tall)
-        cols = slice((s % across) * wide, (s % across + 1) * wide)
-        for k in range(groups - 1):
-            composite[k, rows, cols] = parts[s, k]
-        best[rows, cols] = parts[s, groups - 1].astype(F32).astype(I32)
+    even = (own[0] & 1) == 0
+    for owner in range(2 * slots):
+        rows = slice((owner // across) * tall, (owner // across + 1) * tall)
+        cols = slice((owner % across) * wide, (owner % across + 1) * wide)
+        here = even if owner % 2 == 0 else jnp.logical_not(even)
+        for k in range(groups):
+            part = jnp.where(here, mine[owner // 2, k], other[owner // 2, k])
+            if k < groups - 1:
+                composite[k, rows, cols] = part
+            else:
+                best[rows, cols] = part.astype(F32).astype(I32)
 
 
 def per_device(reflect, quality, instrument_ids, day_of_year, image_rank_values, cloud_penalty):
     dates, rows, cols = quality.shape
     bands = reflect.shape[1]
     sources, chips = lax.axis_size("date"), lax.axis_size("row")
+    own = lax.axis_index("date").astype(I32)[None]
     across = cols // BLOCK
     down = sources // across
     tall = rows // down
@@ -198,7 +221,7 @@
     smem = pl.BlockSpec(memory_space=pltpu.SMEM)
     vmem = pl.BlockSpec(memory_space=pltpu.VMEM)
     hbm = pl.BlockSpec(memory_space=pltpu.HBM)
-    scenes = (instrument_ids, day_of_year, image_rank_values, cloud_penalty)
+    scenes = terms(instrument_ids, day_of_year, image_rank_values, cloud_penalty)
 
     def grant(mib):
         return pltpu.CompilerParams(vmem_limit_bytes=mib << 20)
@@ -220,40 +243,62 @@
     inner_keys, edge_part = pl.pallas_call(
         inner_kernel,
         out_shape=(shape((rows, cols), F32), shape((dates, 2, TILE, cols), F32)),
-        in_specs=[smem] * 4 + [hbm],
+        in_specs=[smem, hbm],
         out_specs=(vmem, vmem),
         scratch_shapes=[pltpu.VMEM((dates, rows, cols), I32), pltpu.SemaphoreType.DMA((dates // GROUP,))],
         compiler_params=grant(BIG),
         name="inner",
-    )(*scenes, quality)
-
-    packed = pl.pallas_call(
+    )(scenes, quality)
+
+    slots = sources // 2
+    packed = shape((slots, bands + 2, tall, BLOCK), BF16)
+    plane = pltpu.VMEM((rows, cols), BF16)
+    keep, send = pl.pallas_call(
         pick_kernel,
-        out_shape=shape((sources, (bands + 2) * tall, BLOCK), BF16),
-        in_specs=[smem] * 4 + [vmem] * 4 + [hbm],
-        out_specs=vmem,
-        scratch_shapes=[pltpu.VMEM((dates, bands, rows, cols), BF16), pltpu.SemaphoreType.DMA((down,))],
+        out_shape=(packed, packed),
+        in_specs=[smem] * 2 + [vmem] * 4 + [hbm],
+        out_specs=(vmem, vmem),
+        scratch_shapes=[
+            pltpu.VMEM((dates, bands, rows, cols), BF16), plane, plane, plane, pltpu.SemaphoreType.DMA((down,))
+        ],
         compiler_params=grant(BIG),
         name="pick",
-    )(*scenes, inner_keys, edge_part, above, below, reflect)
-    arrived = lax.all_to_all(packed, "date", 0, 0, tiled=True)
+    )(own, scenes, inner_keys, edge_part, above, below, reflect)
+    swap = [(z, z ^ 1) for z in range(sources)]
+    alike = [list(range(first, sources, 2)) for first in range(2)]
+
+    def swapped(parts):
+        return lax.ppermute(parts.reshape(-1, BLOCK), "date", swap).reshape(parts.shape)
+
+    def spread_out(parts):
+        flat = parts.reshape(parts.shape[0], -1, BLOCK)
+        return lax.all_to_all(flat, "date", 0, 0, axis_index_groups=alike, tiled=True).reshape(parts.shape)
+
+    paired = pl.pallas_call(
+        pair_kernel,
+        out_shape=packed,
+        in_specs=[vmem, vmem],
+        out_specs=vmem,
+        compiler_params=grant(8),
+        name="pair",
+    )(keep, swapped(send))
     part = pl.pallas_call(
-        functools.partial(merge_kernel, dates),
-        out_shape=shape((sources, bands + 1, tall, BLOCK), BF16),
+        functools.partial(merge_kernel, 2 * dates),
+        out_shape=shape((slots, bands + 1, tall, BLOCK), BF16),
         in_specs=[vmem],
         out_specs=vmem,
         compiler_params=grant(8),
         name="merge",
-    )(arrived.reshape(sources, bands + 2, tall, BLOCK))
-    parts = lax.all_to_all(part.reshape(sources, (bands + 1) * tall, BLOCK), "date", 0, 0, tiled=True)
+    )(spread_out(paired))
+    parts = spread_out(part)
     return pl.pallas_call(
         spread_kernel,
         out_shape=(shape((bands, rows, cols), BF16), shape((rows, cols), I32)),
-        in_specs=[vmem],
+        in_specs=[smem, vmem, vmem],
         out_specs=(vmem, vmem),
         compiler_params=grant(8),
         name="spread",
-    )(parts.reshape(sources, bands + 1, tall, BLOCK))
+    )(own, parts, swapped(parts))
 
 
 def solution(mesh):

time: 115 us -> 103 us (0.90)
  blocking collectives: 92.7 us -> 67.7 us
  waiting for transfers between devices: 0.01 us -> 13.6 us
  Pallas kernels: 14.8 us -> 11.2 us
  starting transfers between devices: 5.91 us -> 8.81 us
    all_to_all x2, blocking collectives: 92.7 us -> 67.7 us  [spread_out(): lax.all_to_all(flat, 'date', 0, 0, axis_index_groups=alike, tiled=True)]
    ppermute x0 -> x2, waiting for transfers between devices: none -> 13.6 us  [swapped(): lax.ppermute(parts.reshape(-1, BLOCK), 'date', swap).reshape(parts.shape)]
    ppermute x0 -> x2, starting transfers between devices: none -> 2.9 us  [swapped(): lax.ppermute(parts.reshape(-1, BLOCK), 'date', swap).reshape(parts.shape)]
    pallas_call x2 -> x3, Pallas kernels: 5.61 us -> 3.85 us  [the longest x1 3.74 us: per_device(): pl.pallas_call(pick_kernel, out_shape=(packed, packed), in_specs=[smem] *...]
    pallas_call x1, Pallas kernels: 5.74 us -> 4.54 us  [per_device(): pl.pallas_call(inner_kernel, out_shape=(shape((rows, cols), F32), shape((...]
  transfers between devices with their start and end apart: 2 -> 4, of which waited for: 0 -> 2; matrix products, arithmetic and copies ran while one was open for 0% -> 1% of each run, Pallas kernels for 5% -> 4%
where the time goes in v3:
time: 103 us
  blocking collectives  67.7 us (66%)
  waiting for transfers between devices  13.6 us (13%)
  Pallas kernels  11.2 us (11%)
  starting transfers between devices  8.81 us (9%)
    all_to_all x2, blocking collectives, spread_out(): lax.all_to_all(flat, 'date', 0, 0, axis_index_groups=alike, tiled=True)  67.7 us
    ppermute x2, waiting for transfers between devices, swapped(): lax.ppermute(parts.reshape(-1, BLOCK), 'date', swap).reshape(parts.shape)  13.6 us
    ppermute x1, starting transfers between devices, per_device(): below = lax.ppermute(first, 'row', [(j, i) for i, j in onward])  4.6 us
    pallas_call x1, Pallas kernels, per_device(): pl.pallas_call(inner_kernel, out_shape=(shape((rows, cols), F32), shape((...  4.54 us
    pallas_call x1, Pallas kernels, per_device(): pl.pallas_call(pick_kernel, out_shape=(packed, packed), in_specs=[smem] *...  3.74 us
    ppermute x2, starting transfers between devices, swapped(): lax.ppermute(parts.reshape(-1, BLOCK), 'date', swap).reshape(parts.shape)  2.9 us
  transfers between devices with their start and end apart: 4, of which 2 were waited for; matrix products, arithmetic and copies ran while one was open for 1% of the time, Pallas kernels for 4%

profile of v3, /device:TPU:38, one launch (start us, length us, event | category | flops | bytes accessed | tf_op | source)
XLA Modules:
  0.0 102.8 jit_solution(1487849435398550031)
XLA Ops:
  0.6 1.9 %edge.1 = (bf16[64,1024]{1,0:T(8,128)(2,1)S(1)}, bf16[64,1024]{1,0:T(8,128)(2,1)S(1)}) custom-call(s32[16,64,1024]{2,1,0:T(8,128)} %words.3), custom_call_target="tpu_custom_call" | custom-call | tf_op jit(solution)/shard_map/edge/pallas_call | solution.py:230
  2.6 1.3 %collective-permute-start = (bf16[64,1024]{1,0:T(8,128)(2,1)S(1)}, bf16[64,1024]{1,0:T(8,128)(2,1)S(1)}, u32[]{:S(2)}, u32[]{:S(2)}) collective-permute-start(bf16[64,1024]{1,0:T(8,128)(2,1)S(1)} %get-tuple-element.10), channel_id=1, source_target_pairs={{0,2},{2,4},{4,6},{1,3},{3,5},{5,7},{8,10},{10,12},{12,14},{9,11},... | collective-permute-start | bytes 393224 | tf_op jit(solution)/shard_map/ppermute | solution.py:240
  3.9 4.6 %collective-permute-start.1 = (bf16[64,1024]{1,0:T(8,128)(2,1)S(1)}, bf16[64,1024]{1,0:T(8,128)(2,1)S(1)}, u32[]{:S(2)}, u32[]{:S(2)}) collective-permute-start(bf16[64,1024]{1,0:T(8,128)(2,1)S(1)} %get-tuple-element.11), channel_id=1, source_target_pairs={{2,0},{4,2},{6,4},{3,1},{5,3},{7,5},{10,8},{12,10},{14,12},{11,9},... | collective-permute-start | bytes 393224 | tf_op jit(solution)/shard_map/ppermute | solution.py:241
  8.5 0.7 iota_add_fusion
  9.2 0.1 add_convert_fusion.scenes
  9.3 4.5 %inner.1 = (f32[64,1024]{1,0:T(8,128)S(1)}, f32[16,2,8,1024]{3,2,1,0:T(8,128)S(1)}) custom-call(f32[32]{0:T(128)S(1)} %add_convert_fusion.scenes, s32[16,64,1024]{2,1,0:T(8,128)} %words.3), custom_call_target="tpu_custom_call" | custom-call | tf_op jit(solution)/shard_map/inner/pallas_call | solution.py:243
  13.9 0.0 collective-permute-done.above
  13.9 0.0 collective-permute-done.1.below
  13.9 3.7 %pick.1 = (bf16[8,5,16,256]{3,2,1,0:T(8,128)(2,1)S(1)}, bf16[8,5,16,256]{3,2,1,0:T(8,128)(2,1)S(1)}) custom-call(s32[1]{0:T(128)} %bitcast.own, f32[32]{0:T(128)S(1)} %add_convert_fusion.scenes, f32[64,1024]{1,0:T(8,128)S(1)} %get-tuple-element.8.keys, f32[16,2,8,1024]{3,2,1,0:T(8,128)S(1)} %get-tuple-element.9.edge, ...), custom_call_target="tpu_custom_call" | custom-call | tf_op jit(solution)/shard_map/pick/pallas_call | solution.py:256
  17.6 2.9 %collective-permute-start.2 = (bf16[640,256]{1,0:T(8,128)(2,1)S(1)}, bf16[640,256]{1,0:T(8,128)(2,1)S(1)}, u32[]{:S(2)}, u32[]{:S(2)}) collective-permute-start(bf16[640,256]{1,0:T(8,128)(2,1)S(1)} %bitcast.16), channel_id=1, source_target_pairs={{0,8},{8,0},{16,24},{24,16},{32,40},{40,32},{48,56},{56,48},{64,72... | collective-permute-start | bytes 983048 | tf_op jit(solution)/shard_map/ppermute | solution.py:271
  20.5 7.2 %collective-permute-done.2 = bf16[640,256]{1,0:T(8,128)(2,1)S(1)} collective-permute-done((bf16[640,256]{1,0:T(8,128)(2,1)S(1)}, bf16[640,256]{1,0:T(8,128)(2,1)S(1)}, u32[]{:S(2)}, u32[]{:S(2)}) %collective-permute-start.2) | collective-permute-done | bytes 327712 | tf_op jit(solution)/shard_map/ppermute | solution.py:271
  27.8 46.0 %all_to_all.10 = bf16[8,80,256]{2,1,0:T(8,128)(2,1)S(1)} all-to-all(bf16[8,80,256]{2,1,0:T(8,128)(2,1)S(1)} %bitcast.10), channel_id=1, replica_groups={{0,16,32,48,64,80,96,112},{8,24,40,56,72,88,104,120},{1,17,33,49,65,81,..., dimensions={0} | all-to-all | bytes 655360 | tf_op jit(solution)/shard_map/all_to_all | solution.py:275
  73.8 0.1 merge.1
  73.8 21.8 %all_to_all.11 = bf16[8,64,256]{2,1,0:T(8,128)(2,1)S(1)} all-to-all(bf16[8,64,256]{2,1,0:T(8,128)(2,1)S(1)} %bitcast.13), channel_id=1, replica_groups={{0,16,32,48,64,80,96,112},{8,24,40,56,72,88,104,120},{1,17,33,49,65,81,..., dimensions={0} | all-to-all | bytes 524288 | tf_op jit(solution)/shard_map/all_to_all | solution.py:275
  95.6 0.0 collective-permute-start.3
  95.6 6.4 %collective-permute-done.3 = bf16[512,256]{1,0:T(8,128)(2,1)S(1)} collective-permute-done((bf16[512,256]{1,0:T(8,128)(2,1)S(1)}, bf16[512,256]{1,0:T(8,128)(2,1)S(1)}, u32[]{:S(2)}, u32[]{:S(2)}) %collective-permute-start.3) | collective-permute-done | bytes 262176 | tf_op jit(solution)/shard_map/ppermute | solution.py:271
  102.0 0.9 spread.1
  (1 shorter events, 0.0 us)
Async XLA Ops:
  2.6 11.3 %collective-permute-start = (bf16[64,1024]{1,0:T(8,128)(2,1)S(1)}, bf16[64,1024]{1,0:T(8,128)(2,1)S(1)}, u32[]{:S(2)}, u32[]{:S(2)}) collective-permute-start(bf16[64,1024]{1,0:T(8,128)(2,1)S(1)} %get-tuple-element.10), channel_id=1, source_target_pairs={{0,2},{2,4},{4,6},{1,3},{3,5},{5,7},{8,10},{10,12},{12,14},{9,11},... | collective-permute-start | bytes 393224 | tf_op jit(solution)/shard_map/ppermute | solution.py:240
  3.9 10.0 %collective-permute-start.1 = (bf16[64,1024]{1,0:T(8,128)(2,1)S(1)}, bf16[64,1024]{1,0:T(8,128)(2,1)S(1)}, u32[]{:S(2)}, u32[]{:S(2)}) collective-permute-start(bf16[64,1024]{1,0:T(8,128)(2,1)S(1)} %get-tuple-element.11), channel_id=1, source_target_pairs={{2,0},{4,2},{6,4},{3,1},{5,3},{7,5},{10,8},{12,10},{14,12},{11,9},... | collective-permute-start | bytes 393224 | tf_op jit(solution)/shard_map/ppermute | solution.py:241
  17.6 10.1 %collective-permute-start.2 = (bf16[640,256]{1,0:T(8,128)(2,1)S(1)}, bf16[640,256]{1,0:T(8,128)(2,1)S(1)}, u32[]{:S(2)}, u32[]{:S(2)}) collective-permute-start(bf16[640,256]{1,0:T(8,128)(2,1)S(1)} %bitcast.16), channel_id=1, source_target_pairs={{0,8},{8,0},{16,24},{24,16},{32,40},{40,32},{48,56},{56,48},{64,72... | collective-permute-start | bytes 983048 | tf_op jit(solution)/shard_map/ppermute | solution.py:271
  95.6 6.4 %collective-permute-start.3 = (bf16[512,256]{1,0:T(8,128)(2,1)S(1)}, bf16[512,256]{1,0:T(8,128)(2,1)S(1)}, u32[]{:S(2)}, u32[]{:S(2)}) collective-permute-start(bf16[512,256]{1,0:T(8,128)(2,1)S(1)} %bitcast.11), channel_id=1, source_target_pairs={{0,8},{8,0},{16,24},{24,16},{32,40},{40,32},{48,56},{56,48},{64,72... | collective-permute-start | bytes 786440 | tf_op jit(solution)/shard_map/ppermute | solution.py:271

commit v4 on v3

--- a/solution.py
+++ b/solution.py
@@ -11,6 +11,7 @@
 TILE = 8
 GROUP = 4
 BLOCK = 256
+LANES = 128
 FLOOR = 126 * 1024
 BIG = 50
 F32 = jnp.float32
@@ -110,10 +111,10 @@
     return (((number & 127) + 128).astype(F32) * power).astype(BF16)
 
 
-def pick_kernel(own, scenes, keys, edge, above, below, reflect, keep, send, near, when, high, low, sems):
+def pick_kernel(own, core, scenes, keys, edge, above, below, reflect, keep, send, cross, away, near, when, high, low, sems):
     dates, bands, rows, cols = reflect.shape
-    across = cols // BLOCK
-    tall = when.shape[0] * across // (2 * keep.shape[0])
+    across = cols // (2 * LANES)
+    tall = keep.shape[2]
     whole = slice(None)
     cuts = [(whole, whole, pl.ds(row, tall)) for row in range(0, rows, tall)]
     copies = fetches(reflect, near, sems, [(cut, cut) for cut in cuts])
@@ -141,9 +142,9 @@
         copy.wait()
         for j in range(across // 2):
             slot = i * (across // 2) + j
-            for side, out in enumerate((keep, send)):
-                col = pl.multiple_of((2 * j + (parity ^ side)) * BLOCK, BLOCK)
-                at = (pl.ds(i * tall, tall), pl.ds(col, BLOCK))
+            for side, half, out in ((1, 1, away), (1, 0, send), (0, 1, cross), (0, 0, keep)):
+                col = pl.multiple_of((4 * j + 2 * (parity ^ side) + (core[0] ^ half)) * LANES, LANES)
+                at = (pl.ds(i * tall, tall), pl.ds(col, LANES))
                 chosen = when[at]
                 hits = [chosen == jnp.asarray(t, BF16) for t in range(dates)]
                 for band in range(bands):
@@ -151,11 +152,12 @@
                     for t in range(1, dates):
                         value = jnp.where(hits[t], near[(t, band, *at)], value)
                     out[slot, band] = value
-                out[slot, bands] = high[at]
-                out[slot, bands + 1] = low[at]
-
-
-def pair_kernel(mine, other, out):
+                if half == 0:
+                    out[slot, bands] = high[at]
+                    out[slot, bands + 1] = low[at]
+
+
+def pair_kernel(mine, mine_rest, other, other_rest, out):
     slots, groups = mine.shape[:2]
     bands = groups - 2
     for s in range(slots):
@@ -163,7 +165,9 @@
         h, l = other[s, bands], other[s, bands + 1]
         better = (h > high) | ((h == high) & (l > low))
         for k in range(groups):
-            out[s, k] = jnp.where(better, other[s, k], mine[s, k])
+            out[s, k if k < bands else k + bands] = jnp.where(better, other[s, k], mine[s, k])
+        for k in range(bands):
+            out[s, bands + k] = jnp.where(better, other_rest[s, k], mine_rest[s, k])
 
 
 def scored(low, dates):
@@ -193,28 +197,38 @@
             out[d, k] = part
 
 
-def spread_kernel(own, mine, other, composite, best):
+def spread_kernel(own, core, mine, swapped, crossed, away, composite, best):
     slots, groups, tall, wide = mine.shape
-    across = best.shape[1] // wide
-    even = (own[0] & 1) == 0
+    bands = composite.shape[0]
+    across = best.shape[1] // (2 * wide)
+    even, first = (own[0] & 1) == 0, core[0] == 0
     for owner in range(2 * slots):
+        s = owner // 2
+        here = even if owner % 2 == 0 else jnp.logical_not(even)
         rows = slice((owner // across) * tall, (owner // across + 1) * tall)
-        cols = slice((owner % across) * wide, (owner % across + 1) * wide)
-        here = even if owner % 2 == 0 else jnp.logical_not(even)
-        for k in range(groups):
-            part = jnp.where(here, mine[owner // 2, k], other[owner // 2, k])
-            if k < groups - 1:
-                composite[k, rows, cols] = part
-            else:
-                best[rows, cols] = part.astype(F32).astype(I32)
+        for half in range(2):
+            start = ((owner % across) * 2 + half) * wide
+            cols = slice(start, start + wide)
+            ours = first if half == 0 else jnp.logical_not(first)
+            for k in range(bands + 1):
+                near, far = (k, bands + k) if k < bands else (groups - 1, groups - 1)
+                part = jnp.where(
+                    ours,
+                    jnp.where(here, mine[s, near], swapped[s, near]),
+                    jnp.where(here, crossed[s, far], away[s, far]),
+                )
+                if k < bands:
+                    composite[k, rows, cols] = part
+                else:
+                    best[rows, cols] = part.astype(F32).astype(I32)
 
 
 def per_device(reflect, quality, instrument_ids, day_of_year, image_rank_values, cloud_penalty):
     dates, rows, cols = quality.shape
     bands = reflect.shape[1]
     sources, chips = lax.axis_size("date"), lax.axis_size("row")
-    own = lax.axis_index("date").astype(I32)[None]
-    across = cols // BLOCK
+    own, core = (lax.axis_index(a).astype(I32)[None] for a in ("date", "band"))
+    across = cols // (2 * LANES)
     down = sources // across
     tall = rows // down
     shape = jax.ShapeDtypeStruct
@@ -251,54 +265,66 @@
     )(scenes, quality)
 
     slots = sources // 2
-    packed = shape((slots, bands + 2, tall, BLOCK), BF16)
+
+    def packed(groups):
+        return shape((slots, groups, tall, LANES), BF16)
+
     plane = pltpu.VMEM((rows, cols), BF16)
-    keep, send = pl.pallas_call(
+    keep, send, cross, away = pl.pallas_call(
         pick_kernel,
-        out_shape=(packed, packed),
-        in_specs=[smem] * 2 + [vmem] * 4 + [hbm],
-        out_specs=(vmem, vmem),
+        out_shape=(packed(bands + 2), packed(bands + 2), packed(bands), packed(bands)),
+        in_specs=[smem] * 3 + [vmem] * 4 + [hbm],
+        out_specs=(vmem,) * 4,
         scratch_shapes=[
             pltpu.VMEM((dates, bands, rows, cols), BF16), plane, plane, plane, pltpu.SemaphoreType.DMA((down,))
         ],
         compiler_params=grant(BIG),
         name="pick",
-    )(own, scenes, inner_keys, edge_part, above, below, reflect)
+    )(own, core, scenes, inner_keys, edge_part, above, below, reflect)
     swap = [(z, z ^ 1) for z in range(sources)]
+    diagonal = [(2 * z + c, 2 * (z ^ 1) + 1 - c) for z in range(sources) for c in range(2)]
     alike = [list(range(first, sources, 2)) for first in range(2)]
 
-    def swapped(parts):
-        return lax.ppermute(parts.reshape(-1, BLOCK), "date", swap).reshape(parts.shape)
+    def moved(parts, axes, pairs):
+        return lax.ppermute(parts.reshape(-1, LANES), axes, pairs).reshape(parts.shape)
+
+    def to_pair(parts):
+        return moved(parts, "date", swap)
+
+    def to_core(parts):
+        return moved(parts, "band", [(0, 1), (1, 0)])
 
     def spread_out(parts):
-        flat = parts.reshape(parts.shape[0], -1, BLOCK)
+        flat = parts.reshape(parts.shape[0], -1, LANES)
         return lax.all_to_all(flat, "date", 0, 0, axis_index_groups=alike, tiled=True).reshape(parts.shape)
 
+    other, other_rest, mine_rest = to_pair(send), moved(away, ("date", "band"), diagonal), to_core(cross)
     paired = pl.pallas_call(
         pair_kernel,
-        out_shape=packed,
-        in_specs=[vmem, vmem],
+        out_shape=packed(2 * bands + 2),
+        in_specs=[vmem] * 4,
         out_specs=vmem,
         compiler_params=grant(8),
         name="pair",
-    )(keep, swapped(send))
+    )(keep, mine_rest, other, other_rest)
     part = pl.pallas_call(
         functools.partial(merge_kernel, 2 * dates),
-        out_shape=shape((slots, bands + 1, tall, BLOCK), BF16),
+        out_shape=packed(2 * bands + 1),
         in_specs=[vmem],
         out_specs=vmem,
         compiler_params=grant(8),
         name="merge",
     )(spread_out(paired))
     parts = spread_out(part)
+    beside = to_pair(parts)
     return pl.pallas_call(
         spread_kernel,
         out_shape=(shape((bands, rows, cols), BF16), shape((rows, cols), I32)),
-        in_specs=[smem, vmem, vmem],
+        in_specs=[smem] * 2 + [vmem] * 4,
         out_specs=(vmem, vmem),
         compiler_params=grant(8),
         name="spread",
-    )(own, parts, swapped(parts))
+    )(own, core, parts, beside, to_core(parts), to_core(beside))
 
 
 def solution(mesh):

time: 103 us -> 101 us (0.981)
  waiting for transfers between devices: 13.6 us -> 11.4 us
  blocking collectives: 67.7 us -> 66.3 us
  starting transfers between devices: 8.81 us -> 9.99 us
    ppermute x2 -> x6, waiting for transfers between devices: 13.6 us -> 11.4 us  [moved(): lax.ppermute(parts.reshape(-1, LANES), axes, pairs).reshape(parts.shape)]
    all_to_all x2, blocking collectives: 67.7 us -> 66.3 us  [spread_out(): lax.all_to_all(flat, 'date', 0, 0, axis_index_groups=alike, tiled=True)]
    ppermute x2 -> x6, starting transfers between devices: 2.9 us -> 4.09 us  [moved(): lax.ppermute(parts.reshape(-1, LANES), axes, pairs).reshape(parts.shape)]
  transfers between devices with their start and end apart: 4 -> 8, of which waited for: 2 -> 4; matrix products, arithmetic and copies ran while one was open for 1% -> 1% of each run, Pallas kernels for 4% -> 5%
where the time goes in v4:
time: 101 us
  blocking collectives  66.3 us (66%)
  Pallas kernels  11.5 us (11%)
  waiting for transfers between devices  11.4 us (11%)
  starting transfers between devices  9.99 us (10%)
    all_to_all x2, blocking collectives, spread_out(): lax.all_to_all(flat, 'date', 0, 0, axis_index_groups=alike, tiled=True)  66.3 us
    ppermute x6, waiting for transfers between devices, moved(): lax.ppermute(parts.reshape(-1, LANES), axes, pairs).reshape(parts.shape)  11.4 us
    ppermute x1, starting transfers between devices, per_device(): below = lax.ppermute(first, 'row', [(j, i) for i, j in onward])  4.6 us
    pallas_call x1, Pallas kernels, per_device(): pl.pallas_call(inner_kernel, out_shape=(shape((rows, cols), F32), shape((...  4.54 us
    ppermute x6, starting transfers between devices, moved(): lax.ppermute(parts.reshape(-1, LANES), axes, pairs).reshape(parts.shape)  4.09 us
    pallas_call x1, Pallas kernels, per_device(): pl.pallas_call(pick_kernel, out_shape=(packed(bands + 2), packed(bands +...  3.95 us
  transfers between devices with their start and end apart: 8, of which 4 were waited for; matrix products, arithmetic and copies ran while one was open for 1% of the time, Pallas kernels for 5%

profile of v4, /device:TPU:38, one launch (start us, length us, event | category | flops | bytes accessed | tf_op | source)
XLA Modules:
  0.0 100.7 jit_solution(4463430244269205494)
XLA Ops:
  0.6 1.9 %edge.1 = (bf16[64,1024]{1,0:T(8,128)(2,1)S(1)}, bf16[64,1024]{1,0:T(8,128)(2,1)S(1)}) custom-call(s32[16,64,1024]{2,1,0:T(8,128)} %words.3), custom_call_target="tpu_custom_call" | custom-call | tf_op jit(solution)/shard_map/edge/pallas_call | solution.py:244
  2.6 1.3 %collective-permute-start = (bf16[64,1024]{1,0:T(8,128)(2,1)S(1)}, bf16[64,1024]{1,0:T(8,128)(2,1)S(1)}, u32[]{:S(2)}, u32[]{:S(2)}) collective-permute-start(bf16[64,1024]{1,0:T(8,128)(2,1)S(1)} %get-tuple-element.12), channel_id=1, source_target_pairs={{0,2},{2,4},{4,6},{1,3},{3,5},{5,7},{8,10},{10,12},{12,14},{9,11},... | collective-permute-start | bytes 393224 | tf_op jit(solution)/shard_map/ppermute | solution.py:254
  3.9 4.6 %collective-permute-start.1 = (bf16[64,1024]{1,0:T(8,128)(2,1)S(1)}, bf16[64,1024]{1,0:T(8,128)(2,1)S(1)}, u32[]{:S(2)}, u32[]{:S(2)}) collective-permute-start(bf16[64,1024]{1,0:T(8,128)(2,1)S(1)} %get-tuple-element.13), channel_id=1, source_target_pairs={{2,0},{4,2},{6,4},{3,1},{5,3},{7,5},{10,8},{12,10},{14,12},{11,9},... | collective-permute-start | bytes 393224 | tf_op jit(solution)/shard_map/ppermute | solution.py:255
  8.5 0.7 iota_add_fusion
  9.2 0.1 add_convert_fusion.scenes
  9.3 4.5 %inner.1 = (f32[64,1024]{1,0:T(8,128)S(1)}, f32[16,2,8,1024]{3,2,1,0:T(8,128)S(1)}) custom-call(f32[32]{0:T(128)S(1)} %add_convert_fusion.scenes, s32[16,64,1024]{2,1,0:T(8,128)} %words.3), custom_call_target="tpu_custom_call" | custom-call | tf_op jit(solution)/shard_map/inner/pallas_call | solution.py:257
  13.9 0.0 collective-permute-done.above
  13.9 0.0 collective-permute-done.1.below
  13.9 3.9 %pick.1 = (bf16[8,5,16,128]{3,2,1,0:T(8,128)(2,1)S(1)}, bf16[8,5,16,128]{3,2,1,0:T(8,128)(2,1)S(1)}, bf16[8,3,16,128]{3,2,1,0:T(8,128)(2,1)S(1)}, bf16[8,3,16,128]{3,2,1,0:T(8,128)(2,1)S(1)}) custom-call(s32[1]{0:T(128)} %bitcast.own, s32[1]{0:T(128)} %bitcast.1.core, f32[32]{0:T(128)S(1)} %add_convert_fusion.scenes, f32[64,1024]{1,0:T(8,128)S(1)} %get-tuple-element.10.keys, ...), custom_call_target="tpu_custom_call" | custom-call | tf_op jit(solution)/shard_map/pick/pallas_call | solution.py:273
  17.8 2.9 %collective-permute-start.3 = (bf16[640,128]{1,0:T(8,128)(2,1)S(1)}, bf16[640,128]{1,0:T(8,128)(2,1)S(1)}, u32[]{:S(2)}, u32[]{:S(2)}) collective-permute-start(bf16[640,128]{1,0:T(8,128)(2,1)S(1)} %bitcast.28), channel_id=1, source_target_pairs={{0,8},{8,0},{16,24},{24,16},{32,40},{40,32},{48,56},{56,48},{64,72... | collective-permute-start | bytes 491528 | tf_op jit(solution)/shard_map/ppermute | solution.py:289
  20.7 0.0 collective-permute-start.2
  20.7 0.3 collective-permute-start.4
  21.0 1.0 %collective-permute-done.2 = bf16[384,128]{1,0:T(8,128)(2,1)S(1)} collective-permute-done((bf16[384,128]{1,0:T(8,128)(2,1)S(1)}, bf16[384,128]{1,0:T(8,128)(2,1)S(1)}, u32[]{:S(2)}, u32[]{:S(2)}) %collective-permute-start.2) | collective-permute-done | bytes 98336 | tf_op jit(solution)/shard_map/ppermute | solution.py:289
  22.0 3.8 %collective-permute-done.4 = bf16[384,128]{1,0:T(8,128)(2,1)S(1)} collective-permute-done((bf16[384,128]{1,0:T(8,128)(2,1)S(1)}, bf16[384,128]{1,0:T(8,128)(2,1)S(1)}, u32[]{:S(2)}, u32[]{:S(2)}) %collective-permute-start.4) | collective-permute-done | bytes 98336 | tf_op jit(solution)/shard_map/ppermute | solution.py:289
  25.8 0.0 collective-permute-done.3
  25.8 0.1 pair.1
  25.9 42.3 %all_to_all.10 = bf16[8,128,128]{2,1,0:T(8,128)(2,1)S(1)} all-to-all(bf16[8,128,128]{2,1,0:T(8,128)(2,1)S(1)} %bitcast.16), channel_id=1, replica_groups={{0,16,32,48,64,80,96,112},{8,24,40,56,72,88,104,120},{1,17,33,49,65,81,..., dimensions={0} | all-to-all | bytes 524288 | tf_op jit(solution)/shard_map/all_to_all | solution.py:299
  68.2 0.1 merge.1
  68.3 23.9 %all_to_all.11 = bf16[8,112,128]{2,1,0:T(8,128)(2,1)S(1)} all-to-all(bf16[8,112,128]{2,1,0:T(8,128)(2,1)S(1)} %bitcast.21), channel_id=1, replica_groups={{0,16,32,48,64,80,96,112},{8,24,40,56,72,88,104,120},{1,17,33,49,65,81,..., dimensions={0} | all-to-all | bytes 458752 | tf_op jit(solution)/shard_map/all_to_all | solution.py:299
  92.2 0.9 collective-permute-start.5
  93.2 0.0 collective-permute-start.6
  93.2 5.1 %collective-permute-done.5 = bf16[896,128]{1,0:T(8,128)(2,1)S(1)} collective-permute-done((bf16[896,128]{1,0:T(8,128)(2,1)S(1)}, bf16[896,128]{1,0:T(8,128)(2,1)S(1)}, u32[]{:S(2)}, u32[]{:S(2)}) %collective-permute-start.5) | collective-permute-done | bytes 229408 | tf_op jit(solution)/shard_map/ppermute | solution.py:289
  98.3 0.0 collective-permute-start.7
  98.3 0.0 collective-permute-done.6
  98.3 1.5 %collective-permute-done.7 = bf16[896,128]{1,0:T(8,128)(2,1)S(1)} collective-permute-done((bf16[896,128]{1,0:T(8,128)(2,1)S(1)}, bf16[896,128]{1,0:T(8,128)(2,1)S(1)}, u32[]{:S(2)}, u32[]{:S(2)}) %collective-permute-start.7) | collective-permute-done | bytes 229408 | tf_op jit(solution)/shard_map/ppermute | solution.py:289
  99.7 0.9 spread.1
Async XLA Ops:
  2.6 11.3 %collective-permute-start = (bf16[64,1024]{1,0:T(8,128)(2,1)S(1)}, bf16[64,1024]{1,0:T(8,128)(2,1)S(1)}, u32[]{:S(2)}, u32[]{:S(2)}) collective-permute-start(bf16[64,1024]{1,0:T(8,128)(2,1)S(1)} %get-tuple-element.12), channel_id=1, source_target_pairs={{0,2},{2,4},{4,6},{1,3},{3,5},{5,7},{8,10},{10,12},{12,14},{9,11},... | collective-permute-start | bytes 393224 | tf_op jit(solution)/shard_map/ppermute | solution.py:254
  3.9 10.0 %collective-permute-start.1 = (bf16[64,1024]{1,0:T(8,128)(2,1)S(1)}, bf16[64,1024]{1,0:T(8,128)(2,1)S(1)}, u32[]{:S(2)}, u32[]{:S(2)}) collective-permute-start(bf16[64,1024]{1,0:T(8,128)(2,1)S(1)} %get-tuple-element.13), channel_id=1, source_target_pairs={{2,0},{4,2},{6,4},{3,1},{5,3},{7,5},{10,8},{12,10},{14,12},{11,9},... | collective-permute-start | bytes 393224 | tf_op jit(solution)/shard_map/ppermute | solution.py:255
  17.8 8.0 %collective-permute-start.3 = (bf16[640,128]{1,0:T(8,128)(2,1)S(1)}, bf16[640,128]{1,0:T(8,128)(2,1)S(1)}, u32[]{:S(2)}, u32[]{:S(2)}) collective-permute-start(bf16[640,128]{1,0:T(8,128)(2,1)S(1)} %bitcast.28), channel_id=1, source_target_pairs={{0,8},{8,0},{16,24},{24,16},{32,40},{40,32},{48,56},{56,48},{64,72... | collective-permute-start | bytes 491528 | tf_op jit(solution)/shard_map/ppermute | solution.py:289
  20.7 1.3 %collective-permute-start.2 = (bf16[384,128]{1,0:T(8,128)(2,1)S(1)}, bf16[384,128]{1,0:T(8,128)(2,1)S(1)}, u32[]{:S(2)}, u32[]{:S(2)}) collective-permute-start(bf16[384,128]{1,0:T(8,128)(2,1)S(1)} %bitcast.30), channel_id=1, source_target_pairs={{0,1},{1,0},{2,3},{3,2},{4,5},{5,4},{6,7},{7,6},{8,9},{9,8},{10,11... | collective-permute-start | bytes 294920 | tf_op jit(solution)/shard_map/ppermute | solution.py:289
  20.7 5.1 %collective-permute-start.4 = (bf16[384,128]{1,0:T(8,128)(2,1)S(1)}, bf16[384,128]{1,0:T(8,128)(2,1)S(1)}, u32[]{:S(2)}, u32[]{:S(2)}) collective-permute-start(bf16[384,128]{1,0:T(8,128)(2,1)S(1)} %bitcast.29), channel_id=1, source_target_pairs={{0,9},{1,8},{8,1},{9,0},{16,25},{17,24},{24,17},{25,16},{32,41},{3... | collective-permute-start | bytes 294920 | tf_op jit(solution)/shard_map/ppermute | solution.py:289
  92.2 6.0 %collective-permute-start.5 = (bf16[896,128]{1,0:T(8,128)(2,1)S(1)}, bf16[896,128]{1,0:T(8,128)(2,1)S(1)}, u32[]{:S(2)}, u32[]{:S(2)}) collective-permute-start(bf16[896,128]{1,0:T(8,128)(2,1)S(1)} %bitcast.18), channel_id=1, source_target_pairs={{0,8},{8,0},{16,24},{24,16},{32,40},{40,32},{48,56},{56,48},{64,72... | collective-permute-start | bytes 688136 | tf_op jit(solution)/shard_map/ppermute | solution.py:289
  93.2 5.1 %collective-permute-start.6 = (bf16[896,128]{1,0:T(8,128)(2,1)S(1)}, bf16[896,128]{1,0:T(8,128)(2,1)S(1)}, u32[]{:S(2)}, u32[]{:S(2)}) collective-permute-start(bf16[896,128]{1,0:T(8,128)(2,1)S(1)} %bitcast.19), channel_id=1, source_target_pairs={{0,1},{1,0},{2,3},{3,2},{4,5},{5,4},{6,7},{7,6},{8,9},{9,8},{10,11... | collective-permute-start | bytes 688136 | tf_op jit(solution)/shard_map/ppermute | solution.py:289
  98.3 1.5 %collective-permute-start.7 = (bf16[896,128]{1,0:T(8,128)(2,1)S(1)}, bf16[896,128]{1,0:T(8,128)(2,1)S(1)}, u32[]{:S(2)}, u32[]{:S(2)}) collective-permute-start(bf16[896,128]{1,0:T(8,128)(2,1)S(1)} %collective-permute-done.5), channel_id=1, source_target_pairs={{0,1},{1,0},{2,3},{3,2},{4,5},{5,4},{6,7},{7,6},{8,9},{9,8},{10,11... | collective-permute-start | bytes 688136 | tf_op jit(solution)/shard_map/ppermute | solution.py:289

commit v5 on v4

--- a/solution.py
+++ b/solution.py
@@ -53,7 +53,7 @@
     season = jnp.minimum(apart, 365 - apart)
     bonus = jnp.where(ids == 1, 300, jnp.where(ids == 2, 500, 0))
     fixed = (16 * ranks + bonus - 4 * season) * dates + jnp.arange(dates, dtype=I32)
-    return jnp.concatenate([fixed, penalties * dates]).astype(F32)
+    return fixed, penalties * dates
 
 
 def fetches(source, target, sems, cuts):
@@ -78,7 +78,7 @@
         out[...] = column_pass(edge)
 
 
-def inner_kernel(scenes, words, keys, edge, near, sems):
+def inner_kernel(bases, slopes, words, keys, edge, near, sems):
     dates, rows, cols = words.shape
     copies = fetches(words, near, sems, [(pl.ds(t, GROUP), pl.ds(t, GROUP)) for t in range(0, dates, GROUP)])
     m, k = iotas((GROUP * rows, GROUP * rows))
@@ -94,7 +94,7 @@
             own = closeness[i * rows : (i + 1) * rows]
             edge[t, 0] = own[:TILE]
             edge[t, 1] = own[rows - TILE :]
-            base, slope = scenes[t], scenes[dates + t]
+            base, slope = bases[t].astype(F32), slopes[t].astype(F32)
             key = base - slope * own
             best = key if best is None else jnp.maximum(best, key)
         keys[...] = best if step == 0 else jnp.maximum(keys[...], best)
@@ -111,17 +111,48 @@
     return (((number & 127) + 128).astype(F32) * power).astype(BF16)
 
 
-def pick_kernel(own, core, scenes, keys, edge, above, below, reflect, keep, send, cross, away, near, when, high, low, sems):
-    dates, bands, rows, cols = reflect.shape
-    across = cols // (2 * LANES)
-    tall = keep.shape[2]
-    whole = slice(None)
-    cuts = [(whole, whole, pl.ds(row, tall)) for row in range(0, rows, tall)]
-    copies = fetches(reflect, near, sems, [(cut, cut) for cut in cuts])
+def blocks(reflect, near, sems, parity):
+    across, whole = near.shape[3] // BLOCK, slice(None)
+    tall = reflect.shape[2] * across // sems.shape[0]
+    cuts = []
+    for i in range(sems.shape[0] // across):
+        for j in range(across):
+            rows, col = pl.ds(i * tall, tall), pl.multiple_of((2 * j + parity) * BLOCK, BLOCK)
+            cuts.append(((whole, whole, rows, pl.ds(col, BLOCK)), (whole, whole, rows, pl.ds(j * BLOCK, BLOCK))))
+    return fetches(reflect, near, sems, cuts)
+
+
+def choose(copies, near, parity, core, codes, coded_out, rest):
+    dates, bands = near.shape[:2]
+    tall = rest.shape[2]
+    across = near.shape[3] // BLOCK
+    for slot, copy in enumerate(copies):
+        copy.wait()
+        i, j = slot // across, slot % across
+        rows = pl.ds(i * tall, tall)
+        for half, out in enumerate((coded_out, rest)):
+            lane = core ^ half
+            at = (rows, pl.ds(pl.multiple_of((4 * j + 2 * parity + lane) * LANES, LANES), LANES))
+            here = (rows, pl.ds(pl.multiple_of((2 * j + lane) * LANES, LANES), LANES))
+            when, high, low = (code[at] for code in codes)
+            hits = [when == jnp.asarray(t, BF16) for t in range(dates)]
+            for band in range(bands):
+                value = near[(0, band, *here)]
+                for t in range(1, dates):
+                    value = jnp.where(hits[t], near[(t, band, *here)], value)
+                out[slot, band] = value
+            if half == 0:
+                out[slot, bands], out[slot, bands + 1] = high, low
+
+
+def first_kernel(own, core, bases, slopes, keys, edge, above, below, reflect, send, away, when, high, low, near, sems):
+    dates = reflect.shape[0]
+    rows = keys.shape[0]
     parity = own[0] & 1
+    copies = blocks(reflect, near, sems, parity ^ 1)
     m, k = iotas((dates * TILE, dates * RADIUS))
     same = m // TILE == k // RADIUS
-    pairs = [(scenes[t], scenes[dates + t]) for t in range(dates)]
+    pairs = [(bases[t].astype(F32), slopes[t].astype(F32)) for t in range(dates)]
     ends = []
     for side, halo, shift in ((0, above, -RADIUS), (1, below, TILE)):
         mix = jnp.where(same, tent(k % RADIUS + shift - m % TILE), 0).astype(F32).astype(BF16)
@@ -138,23 +169,13 @@
     when[...] = small(date)
     high[...] = coded(score >> 3)
     low[...] = small((score & 7) * (2 * dates) + (parity * dates + date))
-    for i, copy in enumerate(copies):
-        copy.wait()
-        for j in range(across // 2):
-            slot = i * (across // 2) + j
-            for side, half, out in ((1, 1, away), (1, 0, send), (0, 1, cross), (0, 0, keep)):
-                col = pl.multiple_of((4 * j + 2 * (parity ^ side) + (core[0] ^ half)) * LANES, LANES)
-                at = (pl.ds(i * tall, tall), pl.ds(col, LANES))
-                chosen = when[at]
-                hits = [chosen == jnp.asarray(t, BF16) for t in range(dates)]
-                for band in range(bands):
-                    value = near[(0, band, *at)]
-                    for t in range(1, dates):
-                        value = jnp.where(hits[t], near[(t, band, *at)], value)
-                    out[slot, band] = value
-                if half == 0:
-                    out[slot, bands] = high[at]
-                    out[slot, bands + 1] = low[at]
+    choose(copies, near, parity ^ 1, core[0], (when, high, low), send, away)
+
+
+def second_kernel(own, core, when, high, low, reflect, keep, cross, near, sems):
+    parity = own[0] & 1
+    copies = blocks(reflect, near, sems, parity)
+    choose(copies, near, parity, core[0], (when, high, low), keep, cross)
 
 
 def pair_kernel(mine, mine_rest, other, other_rest, out):
@@ -257,30 +278,38 @@
     inner_keys, edge_part = pl.pallas_call(
         inner_kernel,
         out_shape=(shape((rows, cols), F32), shape((dates, 2, TILE, cols), F32)),
-        in_specs=[smem, hbm],
+        in_specs=[smem] * 2 + [hbm],
         out_specs=(vmem, vmem),
         scratch_shapes=[pltpu.VMEM((dates, rows, cols), I32), pltpu.SemaphoreType.DMA((dates // GROUP,))],
         compiler_params=grant(BIG),
         name="inner",
-    )(scenes, quality)
+    )(*scenes, quality)
 
     slots = sources // 2
 
     def packed(groups):
         return shape((slots, groups, tall, LANES), BF16)
 
-    plane = pltpu.VMEM((rows, cols), BF16)
-    keep, send, cross, away = pl.pallas_call(
-        pick_kernel,
-        out_shape=(packed(bands + 2), packed(bands + 2), packed(bands), packed(bands)),
-        in_specs=[smem] * 3 + [vmem] * 4 + [hbm],
-        out_specs=(vmem,) * 4,
-        scratch_shapes=[
-            pltpu.VMEM((dates, bands, rows, cols), BF16), plane, plane, plane, pltpu.SemaphoreType.DMA((down,))
-        ],
+    plane = shape((rows, cols), BF16)
+    scratch = [pltpu.VMEM((dates, bands, rows, cols // 2), BF16), pltpu.SemaphoreType.DMA((slots,))]
+    send, away, *codes = pl.pallas_call(
+        first_kernel,
+        out_shape=(packed(bands + 2), packed(bands), plane, plane, plane),
+        in_specs=[smem] * 4 + [vmem] * 4 + [hbm],
+        out_specs=(vmem,) * 5,
+        scratch_shapes=scratch,
         compiler_params=grant(BIG),
-        name="pick",
-    )(own, core, scenes, inner_keys, edge_part, above, below, reflect)
+        name="first",
+    )(own, core, *scenes, inner_keys, edge_part, above, below, reflect)
+    keep, cross = pl.pallas_call(
+        second_kernel,
+        out_shape=(packed(bands + 2), packed(bands)),
+        in_specs=[smem] * 2 + [vmem] * 3 + [hbm],
+        out_specs=(vmem, vmem),
+        scratch_shapes=scratch,
+        compiler_params=grant(BIG),
+        name="second",
+    )(own, core, *codes, reflect)
     swap = [(z, z ^ 1) for z in range(sources)]
     diagonal = [(2 * z + c, 2 * (z ^ 1) + 1 - c) for z in range(sources) for c in range(2)]
     alike = [list(range(first, sources, 2)) for first in range(2)]

time: 101 us -> 100 us (0.990)
  blocking collectives: 66.3 us -> 63.9 us
    all_to_all x2, blocking collectives: 66.3 us -> 63.9 us  [spread_out(): lax.all_to_all(flat, 'date', 0, 0, axis_index_groups=alike, tiled=True)]
    pallas_call x1 -> x2, Pallas kernels: 3.95 us -> 4.59 us  [the longest x1 2.58 us: per_device(): pl.pallas_call(first_kernel, out_shape=(packed(bands + 2), packed(bands),...]
  transfers between devices with their start and end apart: 8 -> 8, of which waited for: 4 -> 4; matrix products, arithmetic and copies ran while one was open for 1% -> 1% of each run, Pallas kernels for 5% -> 7%
where the time goes in v5:
time: 100 us; the launch traced here: 99.6 us
  blocking collectives  63.9 us (64%)
  Pallas kernels  12.2 us (12%)
  waiting for transfers between devices  12.1 us (12%)
  starting transfers between devices  10 us (10%)
    all_to_all x2, blocking collectives, spread_out(): lax.all_to_all(flat, 'date', 0, 0, axis_index_groups=alike, tiled=True)  63.9 us
    ppermute x6, waiting for transfers between devices, moved(): lax.ppermute(parts.reshape(-1, LANES), axes, pairs).reshape(parts.shape)  12.1 us
    ppermute x1, starting transfers between devices, per_device(): below = lax.ppermute(first, 'row', [(j, i) for i, j in onward])  4.6 us
    pallas_call x1, Pallas kernels, per_device(): pl.pallas_call(inner_kernel, out_shape=(shape((rows, cols), F32), shape((...  4.54 us
    ppermute x6, starting transfers between devices, moved(): lax.ppermute(parts.reshape(-1, LANES), axes, pairs).reshape(parts.shape)  4.1 us
    pallas_call x1, Pallas kernels, per_device(): pl.pallas_call(first_kernel, out_shape=(packed(bands + 2), packed(bands),...  2.58 us
    pallas_call x1, Pallas kernels, per_device(): pl.pallas_call(second_kernel, out_shape=(packed(bands + 2), packed(bands)...  2.01 us
  transfers between devices with their start and end apart: 8, of which 4 were waited for; matrix products, arithmetic and copies ran while one was open for 1% of the time, Pallas kernels for 7%

profile of v5, /device:TPU:38, one launch (start us, length us, event | category | flops | bytes accessed | tf_op | source)
XLA Modules:
  0.0 99.6 jit_solution(14700764978419833876)
XLA Ops:
  0.6 1.9 %edge.1 = (bf16[64,1024]{1,0:T(8,128)(2,1)S(1)}, bf16[64,1024]{1,0:T(8,128)(2,1)S(1)}) custom-call(s32[16,64,1024]{2,1,0:T(8,128)} %words.3), custom_call_target="tpu_custom_call" | custom-call | tf_op jit(solution)/shard_map/edge/pallas_call | solution.py:265
  2.6 1.3 %collective-permute-start = (bf16[64,1024]{1,0:T(8,128)(2,1)S(1)}, bf16[64,1024]{1,0:T(8,128)(2,1)S(1)}, u32[]{:S(2)}, u32[]{:S(2)}) collective-permute-start(bf16[64,1024]{1,0:T(8,128)(2,1)S(1)} %get-tuple-element.15), channel_id=1, source_target_pairs={{0,2},{2,4},{4,6},{1,3},{3,5},{5,7},{8,10},{10,12},{12,14},{9,11},... | collective-permute-start | bytes 393224 | tf_op jit(solution)/shard_map/ppermute | solution.py:275
  3.9 4.6 %collective-permute-start.1 = (bf16[64,1024]{1,0:T(8,128)(2,1)S(1)}, bf16[64,1024]{1,0:T(8,128)(2,1)S(1)}, u32[]{:S(2)}, u32[]{:S(2)}) collective-permute-start(bf16[64,1024]{1,0:T(8,128)(2,1)S(1)} %get-tuple-element.16), channel_id=1, source_target_pairs={{2,0},{4,2},{6,4},{3,1},{5,3},{7,5},{10,8},{12,10},{14,12},{11,9},... | collective-permute-start | bytes 393224 | tf_op jit(solution)/shard_map/ppermute | solution.py:276
  8.5 0.7 iota_add_fusion
  9.2 4.5 %inner.1 = (f32[64,1024]{1,0:T(8,128)S(1)}, f32[16,2,8,1024]{3,2,1,0:T(8,128)S(1)}) custom-call(s32[16]{0:T(128)S(1)} %get-tuple-element.24.bases, s32[16]{0:T(128)S(1)} %get-tuple-element.25.slopes, s32[16,64,1024]{2,1,0:T(8,128)} %words.3), custom_call_target="tpu_custom_call" | custom-call | tf_op jit(solution)/shard_map/inner/pallas_call | solution.py:278
  13.8 0.0 collective-permute-done.above
  13.8 0.0 collective-permute-done.1.below
  13.8 2.6 %first.1 = (bf16[8,5,16,128]{3,2,1,0:T(8,128)(2,1)S(1)}, bf16[8,3,16,128]{3,2,1,0:T(8,128)(2,1)S(1)}, bf16[64,1024]{1,0:T(8,128)(2,1)S(1)}, bf16[64,1024]{1,0:T(8,128)(2,1)S(1)}, bf16[64,1024]{1,0:T(8,128)(2,1)S(1)}) custom-call(s32[1]{0:T(128)} %bitcast.own, s32[1]{0:T(128)} %bitcast.1.core, s32[16]{0:T(128)S(1)} %get-tuple-element.24.bases, ...), custom_call_target="tpu_custom_call" | custom-call | tf_op jit(solution)/shard_map/first/pallas_call | solution.py:295
  16.4 2.9 %collective-permute-start.3 = (bf16[640,128]{1,0:T(8,128)(2,1)S(1)}, bf16[640,128]{1,0:T(8,128)(2,1)S(1)}, u32[]{:S(2)}, u32[]{:S(2)}) collective-permute-start(bf16[640,128]{1,0:T(8,128)(2,1)S(1)} %bitcast.28), channel_id=1, source_target_pairs={{0,8},{8,0},{16,24},{24,16},{32,40},{40,32},{48,56},{56,48},{64,72... | collective-permute-start | bytes 491528 | tf_op jit(solution)/shard_map/ppermute | solution.py:318
  19.3 2.0 %second.1 = (bf16[8,5,16,128]{3,2,1,0:T(8,128)(2,1)S(1)}, bf16[8,3,16,128]{3,2,1,0:T(8,128)(2,1)S(1)}) custom-call(s32[1]{0:T(128)} %bitcast.own, s32[1]{0:T(128)} %bitcast.1.core, bf16[64,1024]{1,0:T(8,128)(2,1)S(1)} %get-tuple-element.17.when, bf16[64,1024]{1,0:T(8,128)(2,1)S(1)} %get-tuple-element.18.high, bf16[64,1024]{1,0:T(8,128)(2,1)S(1)} %get-tuple-element.19.low, ...), custom_call_target="tpu_custom_call" | custom-call | tf_op jit(solution)/shard_map/second/pallas_call | solution.py:304
  21.3 0.1 collective-permute-start.2
  21.5 0.1 collective-permute-start.4
  21.6 1.1 %collective-permute-done.2 = bf16[384,128]{1,0:T(8,128)(2,1)S(1)} collective-permute-done((bf16[384,128]{1,0:T(8,128)(2,1)S(1)}, bf16[384,128]{1,0:T(8,128)(2,1)S(1)}, u32[]{:S(2)}, u32[]{:S(2)}) %collective-permute-start.2) | collective-permute-done | bytes 98336 | tf_op jit(solution)/shard_map/ppermute | solution.py:318
  22.7 3.4 %collective-permute-done.4 = bf16[384,128]{1,0:T(8,128)(2,1)S(1)} collective-permute-done((bf16[384,128]{1,0:T(8,128)(2,1)S(1)}, bf16[384,128]{1,0:T(8,128)(2,1)S(1)}, u32[]{:S(2)}, u32[]{:S(2)}) %collective-permute-start.4) | collective-permute-done | bytes 98336 | tf_op jit(solution)/shard_map/ppermute | solution.py:318
  26.1 0.0 collective-permute-done.3
  26.1 0.1 pair.1
  26.2 43.3 %all_to_all.10 = bf16[8,128,128]{2,1,0:T(8,128)(2,1)S(1)} all-to-all(bf16[8,128,128]{2,1,0:T(8,128)(2,1)S(1)} %bitcast.16), channel_id=1, replica_groups={{0,16,32,48,64,80,96,112},{8,24,40,56,72,88,104,120},{1,17,33,49,65,81,..., dimensions={0} | all-to-all | bytes 524288 | tf_op jit(solution)/shard_map/all_to_all | solution.py:328
  69.5 0.1 merge.1
  69.6 20.6 %all_to_all.11 = bf16[8,112,128]{2,1,0:T(8,128)(2,1)S(1)} all-to-all(bf16[8,112,128]{2,1,0:T(8,128)(2,1)S(1)} %bitcast.21), channel_id=1, replica_groups={{0,16,32,48,64,80,96,112},{8,24,40,56,72,88,104,120},{1,17,33,49,65,81,..., dimensions={0} | all-to-all | bytes 458752 | tf_op jit(solution)/shard_map/all_to_all | solution.py:328
  90.2 0.9 collective-permute-start.5
  91.1 0.0 collective-permute-start.6
  91.1 6.1 %collective-permute-done.5 = bf16[896,128]{1,0:T(8,128)(2,1)S(1)} collective-permute-done((bf16[896,128]{1,0:T(8,128)(2,1)S(1)}, bf16[896,128]{1,0:T(8,128)(2,1)S(1)}, u32[]{:S(2)}, u32[]{:S(2)}) %collective-permute-start.5) | collective-permute-done | bytes 229408 | tf_op jit(solution)/shard_map/ppermute | solution.py:318
  97.1 0.0 collective-permute-start.7
  97.1 0.0 collective-permute-done.6
  97.1 1.5 %collective-permute-done.7 = bf16[896,128]{1,0:T(8,128)(2,1)S(1)} collective-permute-done((bf16[896,128]{1,0:T(8,128)(2,1)S(1)}, bf16[896,128]{1,0:T(8,128)(2,1)S(1)}, u32[]{:S(2)}, u32[]{:S(2)}) %collective-permute-start.7) | collective-permute-done | bytes 229408 | tf_op jit(solution)/shard_map/ppermute | solution.py:318
  98.6 0.9 spread.1
Async XLA Ops:
  2.6 11.2 %collective-permute-start = (bf16[64,1024]{1,0:T(8,128)(2,1)S(1)}, bf16[64,1024]{1,0:T(8,128)(2,1)S(1)}, u32[]{:S(2)}, u32[]{:S(2)}) collective-permute-start(bf16[64,1024]{1,0:T(8,128)(2,1)S(1)} %get-tuple-element.15), channel_id=1, source_target_pairs={{0,2},{2,4},{4,6},{1,3},{3,5},{5,7},{8,10},{10,12},{12,14},{9,11},... | collective-permute-start | bytes 393224 | tf_op jit(solution)/shard_map/ppermute | solution.py:275
  3.9 9.9 %collective-permute-start.1 = (bf16[64,1024]{1,0:T(8,128)(2,1)S(1)}, bf16[64,1024]{1,0:T(8,128)(2,1)S(1)}, u32[]{:S(2)}, u32[]{:S(2)}) collective-permute-start(bf16[64,1024]{1,0:T(8,128)(2,1)S(1)} %get-tuple-element.16), channel_id=1, source_target_pairs={{2,0},{4,2},{6,4},{3,1},{5,3},{7,5},{10,8},{12,10},{14,12},{11,9},... | collective-permute-start | bytes 393224 | tf_op jit(solution)/shard_map/ppermute | solution.py:276
  16.4 9.7 %collective-permute-start.3 = (bf16[640,128]{1,0:T(8,128)(2,1)S(1)}, bf16[640,128]{1,0:T(8,128)(2,1)S(1)}, u32[]{:S(2)}, u32[]{:S(2)}) collective-permute-start(bf16[640,128]{1,0:T(8,128)(2,1)S(1)} %bitcast.28), channel_id=1, source_target_pairs={{0,8},{8,0},{16,24},{24,16},{32,40},{40,32},{48,56},{56,48},{64,72... | collective-permute-start | bytes 491528 | tf_op jit(solution)/shard_map/ppermute | solution.py:318
  21.3 1.4 %collective-permute-start.2 = (bf16[384,128]{1,0:T(8,128)(2,1)S(1)}, bf16[384,128]{1,0:T(8,128)(2,1)S(1)}, u32[]{:S(2)}, u32[]{:S(2)}) collective-permute-start(bf16[384,128]{1,0:T(8,128)(2,1)S(1)} %bitcast.30), channel_id=1, source_target_pairs={{0,1},{1,0},{2,3},{3,2},{4,5},{5,4},{6,7},{7,6},{8,9},{9,8},{10,11... | collective-permute-start | bytes 294920 | tf_op jit(solution)/shard_map/ppermute | solution.py:318
  21.5 4.7 %collective-permute-start.4 = (bf16[384,128]{1,0:T(8,128)(2,1)S(1)}, bf16[384,128]{1,0:T(8,128)(2,1)S(1)}, u32[]{:S(2)}, u32[]{:S(2)}) collective-permute-start(bf16[384,128]{1,0:T(8,128)(2,1)S(1)} %bitcast.29), channel_id=1, source_target_pairs={{0,9},{1,8},{8,1},{9,0},{16,25},{17,24},{24,17},{25,16},{32,41},{3... | collective-permute-start | bytes 294920 | tf_op jit(solution)/shard_map/ppermute | solution.py:318
  90.2 7.0 %collective-permute-start.5 = (bf16[896,128]{1,0:T(8,128)(2,1)S(1)}, bf16[896,128]{1,0:T(8,128)(2,1)S(1)}, u32[]{:S(2)}, u32[]{:S(2)}) collective-permute-start(bf16[896,128]{1,0:T(8,128)(2,1)S(1)} %bitcast.18), channel_id=1, source_target_pairs={{0,8},{8,0},{16,24},{24,16},{32,40},{40,32},{48,56},{56,48},{64,72... | collective-permute-start | bytes 688136 | tf_op jit(solution)/shard_map/ppermute | solution.py:318
  91.1 6.1 %collective-permute-start.6 = (bf16[896,128]{1,0:T(8,128)(2,1)S(1)}, bf16[896,128]{1,0:T(8,128)(2,1)S(1)}, u32[]{:S(2)}, u32[]{:S(2)}) collective-permute-start(bf16[896,128]{1,0:T(8,128)(2,1)S(1)} %bitcast.19), channel_id=1, source_target_pairs={{0,1},{1,0},{2,3},{3,2},{4,5},{5,4},{6,7},{7,6},{8,9},{9,8},{10,11... | collective-permute-start | bytes 688136 | tf_op jit(solution)/shard_map/ppermute | solution.py:318
  97.1 1.5 %collective-permute-start.7 = (bf16[896,128]{1,0:T(8,128)(2,1)S(1)}, bf16[896,128]{1,0:T(8,128)(2,1)S(1)}, u32[]{:S(2)}, u32[]{:S(2)}) collective-permute-start(bf16[896,128]{1,0:T(8,128)(2,1)S(1)} %collective-permute-done.5), channel_id=1, source_target_pairs={{0,1},{1,0},{2,3},{3,2},{4,5},{5,4},{6,7},{7,6},{8,9},{9,8},{10,11... | collective-permute-start | bytes 688136 | tf_op jit(solution)/shard_map/ppermute | solution.py:318

commit v6 on v5

--- a/solution.py
+++ b/solution.py
@@ -28,8 +28,8 @@
 
 
 def obstruction(words):
-    level = ((words >> 8) & 3) + ((words >> 10) & 3)
-    return level.astype(F32)
+    pair = (words >> 8) & 15
+    return ((pair & 3) + (pair >> 2)).astype(F32)
 
 
 def column_pass(blocked):
@@ -65,17 +65,20 @@
 
 def edge_kernel(words, first, last, near, sems):
     dates, rows, _ = words.shape
-    row, col = iotas((dates * RADIUS, dates * TILE))
     whole = slice(None)
     cuts = [((whole, pl.ds(start, TILE)), side) for side, start in enumerate((0, rows - TILE))]
     copies = fetches(words, near, sems, cuts)
-    for side, (out, shift) in enumerate(((first, 0), (last, TILE - RADIUS))):
-        wanted = (row // RADIUS) * TILE + row % RADIUS + shift
-        pick = (wanted == col).astype(F32).astype(BF16)
-        copies[side].wait()
-        level = obstruction(near[side]).reshape(dates * TILE, -1).astype(BF16)
-        edge = jnp.dot(pick, level, preferred_element_type=F32).astype(BF16)
-        out[...] = column_pass(edge)
+    sent = dates * RADIUS
+    row, col = iotas((2 * sent, 2 * dates * TILE))
+    wanted = (row // RADIUS) * TILE + row % RADIUS + (row // sent) * (TILE - RADIUS)
+    pick = (wanted == col).astype(F32).astype(BF16)
+    for copy in copies:
+        copy.wait()
+    level = obstruction(near[...]).reshape(2 * dates * TILE, -1).astype(BF16)
+    edge = jnp.dot(pick, level, preferred_element_type=F32).astype(BF16)
+    across = column_pass(edge)
+    first[...] = across[:sent]
+    last[...] = across[sent:]
 
 
 def inner_kernel(bases, slopes, words, keys, edge, near, sems):

time: 100 us -> 100 us (level)
  no operation moved by 1% of the time
where the time goes in v6:
time: 100 us; the launch traced here: 99.5 us
  blocking collectives  63.9 us (64%)
  Pallas kernels  12.1 us (12%)
  waiting for transfers between devices  12.1 us (12%)
  starting transfers between devices  10 us (10%)
    all_to_all x2, blocking collectives, spread_out(): lax.all_to_all(flat, 'date', 0, 0, axis_index_groups=alike, tiled=True)  63.9 us
    ppermute x6, waiting for transfers between devices, moved(): lax.ppermute(parts.reshape(-1, LANES), axes, pairs).reshape(parts.shape)  12.1 us
    ppermute x1, starting transfers between devices, per_device(): below = lax.ppermute(first, 'row', [(j, i) for i, j in onward])  4.6 us
    pallas_call x1, Pallas kernels, per_device(): pl.pallas_call(inner_kernel, out_shape=(shape((rows, cols), F32), shape((...  4.56 us
    ppermute x6, starting transfers between devices, moved(): lax.ppermute(parts.reshape(-1, LANES), axes, pairs).reshape(parts.shape)  4.1 us
    pallas_call x1, Pallas kernels, per_device(): pl.pallas_call(first_kernel, out_shape=(packed(bands + 2), packed(bands),...  2.58 us
    pallas_call x1, Pallas kernels, per_device(): pl.pallas_call(second_kernel, out_shape=(packed(bands + 2), packed(bands)...  2.01 us
  transfers between devices with their start and end apart: 8, of which 4 were waited for; matrix products, arithmetic and copies ran while one was open for 1% of the time, Pallas kernels for 7%

profile of v6, /device:TPU:38, one launch (start us, length us, event | category | flops | bytes accessed | tf_op | source)
XLA Modules:
  0.0 99.5 jit_solution(9816883066732297334)
XLA Ops:
  0.6 1.9 %edge.1 = (bf16[64,1024]{1,0:T(8,128)(2,1)S(1)}, bf16[64,1024]{1,0:T(8,128)(2,1)S(1)}) custom-call(s32[16,64,1024]{2,1,0:T(8,128)} %words.3), custom_call_target="tpu_custom_call" | custom-call | tf_op jit(solution)/shard_map/edge/pallas_call | solution.py:268
  2.5 1.3 %collective-permute-start = (bf16[64,1024]{1,0:T(8,128)(2,1)S(1)}, bf16[64,1024]{1,0:T(8,128)(2,1)S(1)}, u32[]{:S(2)}, u32[]{:S(2)}) collective-permute-start(bf16[64,1024]{1,0:T(8,128)(2,1)S(1)} %get-tuple-element.15), channel_id=1, source_target_pairs={{0,2},{2,4},{4,6},{1,3},{3,5},{5,7},{8,10},{10,12},{12,14},{9,11},... | collective-permute-start | bytes 393224 | tf_op jit(solution)/shard_map/ppermute | solution.py:278
  3.8 4.6 %collective-permute-start.1 = (bf16[64,1024]{1,0:T(8,128)(2,1)S(1)}, bf16[64,1024]{1,0:T(8,128)(2,1)S(1)}, u32[]{:S(2)}, u32[]{:S(2)}) collective-permute-start(bf16[64,1024]{1,0:T(8,128)(2,1)S(1)} %get-tuple-element.16), channel_id=1, source_target_pairs={{2,0},{4,2},{6,4},{3,1},{5,3},{7,5},{10,8},{12,10},{14,12},{11,9},... | collective-permute-start | bytes 393224 | tf_op jit(solution)/shard_map/ppermute | solution.py:279
  8.4 0.7 iota_add_fusion
  9.1 4.6 %inner.1 = (f32[64,1024]{1,0:T(8,128)S(1)}, f32[16,2,8,1024]{3,2,1,0:T(8,128)S(1)}) custom-call(s32[16]{0:T(128)S(1)} %get-tuple-element.24.bases, s32[16]{0:T(128)S(1)} %get-tuple-element.25.slopes, s32[16,64,1024]{2,1,0:T(8,128)} %words.3), custom_call_target="tpu_custom_call" | custom-call | tf_op jit(solution)/shard_map/inner/pallas_call | solution.py:281
  13.7 0.0 collective-permute-done.above
  13.7 0.0 collective-permute-done.1.below
  13.7 2.6 %first.1 = (bf16[8,5,16,128]{3,2,1,0:T(8,128)(2,1)S(1)}, bf16[8,3,16,128]{3,2,1,0:T(8,128)(2,1)S(1)}, bf16[64,1024]{1,0:T(8,128)(2,1)S(1)}, bf16[64,1024]{1,0:T(8,128)(2,1)S(1)}, bf16[64,1024]{1,0:T(8,128)(2,1)S(1)}) custom-call(s32[1]{0:T(128)} %bitcast.own, s32[1]{0:T(128)} %bitcast.1.core, s32[16]{0:T(128)S(1)} %get-tuple-element.24.bases, ...), custom_call_target="tpu_custom_call" | custom-call | tf_op jit(solution)/shard_map/first/pallas_call | solution.py:298
  16.3 2.9 %collective-permute-start.3 = (bf16[640,128]{1,0:T(8,128)(2,1)S(1)}, bf16[640,128]{1,0:T(8,128)(2,1)S(1)}, u32[]{:S(2)}, u32[]{:S(2)}) collective-permute-start(bf16[640,128]{1,0:T(8,128)(2,1)S(1)} %bitcast.28), channel_id=1, source_target_pairs={{0,8},{8,0},{16,24},{24,16},{32,40},{40,32},{48,56},{56,48},{64,72... | collective-permute-start | bytes 491528 | tf_op jit(solution)/shard_map/ppermute | solution.py:321
  19.2 2.0 %second.1 = (bf16[8,5,16,128]{3,2,1,0:T(8,128)(2,1)S(1)}, bf16[8,3,16,128]{3,2,1,0:T(8,128)(2,1)S(1)}) custom-call(s32[1]{0:T(128)} %bitcast.own, s32[1]{0:T(128)} %bitcast.1.core, bf16[64,1024]{1,0:T(8,128)(2,1)S(1)} %get-tuple-element.17.when, bf16[64,1024]{1,0:T(8,128)(2,1)S(1)} %get-tuple-element.18.high, bf16[64,1024]{1,0:T(8,128)(2,1)S(1)} %get-tuple-element.19.low, ...), custom_call_target="tpu_custom_call" | custom-call | tf_op jit(solution)/shard_map/second/pallas_call | solution.py:307
  21.2 0.1 collective-permute-start.2
  21.4 0.1 collective-permute-start.4
  21.5 1.1 %collective-permute-done.2 = bf16[384,128]{1,0:T(8,128)(2,1)S(1)} collective-permute-done((bf16[384,128]{1,0:T(8,128)(2,1)S(1)}, bf16[384,128]{1,0:T(8,128)(2,1)S(1)}, u32[]{:S(2)}, u32[]{:S(2)}) %collective-permute-start.2) | collective-permute-done | bytes 98336 | tf_op jit(solution)/shard_map/ppermute | solution.py:321
  22.7 3.4 %collective-permute-done.4 = bf16[384,128]{1,0:T(8,128)(2,1)S(1)} collective-permute-done((bf16[384,128]{1,0:T(8,128)(2,1)S(1)}, bf16[384,128]{1,0:T(8,128)(2,1)S(1)}, u32[]{:S(2)}, u32[]{:S(2)}) %collective-permute-start.4) | collective-permute-done | bytes 98336 | tf_op jit(solution)/shard_map/ppermute | solution.py:321
  26.1 0.0 collective-permute-done.3
  26.1 0.1 pair.1
  26.1 43.3 %all_to_all.10 = bf16[8,128,128]{2,1,0:T(8,128)(2,1)S(1)} all-to-all(bf16[8,128,128]{2,1,0:T(8,128)(2,1)S(1)} %bitcast.16), channel_id=1, replica_groups={{0,16,32,48,64,80,96,112},{8,24,40,56,72,88,104,120},{1,17,33,49,65,81,..., dimensions={0} | all-to-all | bytes 524288 | tf_op jit(solution)/shard_map/all_to_all | solution.py:331
  69.5 0.1 merge.1
  69.5 20.6 %all_to_all.11 = bf16[8,112,128]{2,1,0:T(8,128)(2,1)S(1)} all-to-all(bf16[8,112,128]{2,1,0:T(8,128)(2,1)S(1)} %bitcast.21), channel_id=1, replica_groups={{0,16,32,48,64,80,96,112},{8,24,40,56,72,88,104,120},{1,17,33,49,65,81,..., dimensions={0} | all-to-all | bytes 458752 | tf_op jit(solution)/shard_map/all_to_all | solution.py:331
  90.1 0.9 collective-permute-start.5
  91.0 0.0 collective-permute-start.6
  91.0 6.1 %collective-permute-done.5 = bf16[896,128]{1,0:T(8,128)(2,1)S(1)} collective-permute-done((bf16[896,128]{1,0:T(8,128)(2,1)S(1)}, bf16[896,128]{1,0:T(8,128)(2,1)S(1)}, u32[]{:S(2)}, u32[]{:S(2)}) %collective-permute-start.5) | collective-permute-done | bytes 229408 | tf_op jit(solution)/shard_map/ppermute | solution.py:321
  97.1 0.0 collective-permute-start.7
  97.1 0.0 collective-permute-done.6
  97.1 1.5 %collective-permute-done.7 = bf16[896,128]{1,0:T(8,128)(2,1)S(1)} collective-permute-done((bf16[896,128]{1,0:T(8,128)(2,1)S(1)}, bf16[896,128]{1,0:T(8,128)(2,1)S(1)}, u32[]{:S(2)}, u32[]{:S(2)}) %collective-permute-start.7) | collective-permute-done | bytes 229408 | tf_op jit(solution)/shard_map/ppermute | solution.py:321
  98.5 0.9 spread.1
Async XLA Ops:
  2.5 11.2 %collective-permute-start = (bf16[64,1024]{1,0:T(8,128)(2,1)S(1)}, bf16[64,1024]{1,0:T(8,128)(2,1)S(1)}, u32[]{:S(2)}, u32[]{:S(2)}) collective-permute-start(bf16[64,1024]{1,0:T(8,128)(2,1)S(1)} %get-tuple-element.15), channel_id=1, source_target_pairs={{0,2},{2,4},{4,6},{1,3},{3,5},{5,7},{8,10},{10,12},{12,14},{9,11},... | collective-permute-start | bytes 393224 | tf_op jit(solution)/shard_map/ppermute | solution.py:278
  3.8 9.9 %collective-permute-start.1 = (bf16[64,1024]{1,0:T(8,128)(2,1)S(1)}, bf16[64,1024]{1,0:T(8,128)(2,1)S(1)}, u32[]{:S(2)}, u32[]{:S(2)}) collective-permute-start(bf16[64,1024]{1,0:T(8,128)(2,1)S(1)} %get-tuple-element.16), channel_id=1, source_target_pairs={{2,0},{4,2},{6,4},{3,1},{5,3},{7,5},{10,8},{12,10},{14,12},{11,9},... | collective-permute-start | bytes 393224 | tf_op jit(solution)/shard_map/ppermute | solution.py:279
  16.3 9.7 %collective-permute-start.3 = (bf16[640,128]{1,0:T(8,128)(2,1)S(1)}, bf16[640,128]{1,0:T(8,128)(2,1)S(1)}, u32[]{:S(2)}, u32[]{:S(2)}) collective-permute-start(bf16[640,128]{1,0:T(8,128)(2,1)S(1)} %bitcast.28), channel_id=1, source_target_pairs={{0,8},{8,0},{16,24},{24,16},{32,40},{40,32},{48,56},{56,48},{64,72... | collective-permute-start | bytes 491528 | tf_op jit(solution)/shard_map/ppermute | solution.py:321
  21.2 1.4 %collective-permute-start.2 = (bf16[384,128]{1,0:T(8,128)(2,1)S(1)}, bf16[384,128]{1,0:T(8,128)(2,1)S(1)}, u32[]{:S(2)}, u32[]{:S(2)}) collective-permute-start(bf16[384,128]{1,0:T(8,128)(2,1)S(1)} %bitcast.30), channel_id=1, source_target_pairs={{0,1},{1,0},{2,3},{3,2},{4,5},{5,4},{6,7},{7,6},{8,9},{9,8},{10,11... | collective-permute-start | bytes 294920 | tf_op jit(solution)/shard_map/ppermute | solution.py:321
  21.4 4.7 %collective-permute-start.4 = (bf16[384,128]{1,0:T(8,128)(2,1)S(1)}, bf16[384,128]{1,0:T(8,128)(2,1)S(1)}, u32[]{:S(2)}, u32[]{:S(2)}) collective-permute-start(bf16[384,128]{1,0:T(8,128)(2,1)S(1)} %bitcast.29), channel_id=1, source_target_pairs={{0,9},{1,8},{8,1},{9,0},{16,25},{17,24},{24,17},{25,16},{32,41},{3... | collective-permute-start | bytes 294920 | tf_op jit(solution)/shard_map/ppermute | solution.py:321
  90.1 7.0 %collective-permute-start.5 = (bf16[896,128]{1,0:T(8,128)(2,1)S(1)}, bf16[896,128]{1,0:T(8,128)(2,1)S(1)}, u32[]{:S(2)}, u32[]{:S(2)}) collective-permute-start(bf16[896,128]{1,0:T(8,128)(2,1)S(1)} %bitcast.18), channel_id=1, source_target_pairs={{0,8},{8,0},{16,24},{24,16},{32,40},{40,32},{48,56},{56,48},{64,72... | collective-permute-start | bytes 688136 | tf_op jit(solution)/shard_map/ppermute | solution.py:321
  91.0 6.1 %collective-permute-start.6 = (bf16[896,128]{1,0:T(8,128)(2,1)S(1)}, bf16[896,128]{1,0:T(8,128)(2,1)S(1)}, u32[]{:S(2)}, u32[]{:S(2)}) collective-permute-start(bf16[896,128]{1,0:T(8,128)(2,1)S(1)} %bitcast.19), channel_id=1, source_target_pairs={{0,1},{1,0},{2,3},{3,2},{4,5},{5,4},{6,7},{7,6},{8,9},{9,8},{10,11... | collective-permute-start | bytes 688136 | tf_op jit(solution)/shard_map/ppermute | solution.py:321
  97.1 1.5 %collective-permute-start.7 = (bf16[896,128]{1,0:T(8,128)(2,1)S(1)}, bf16[896,128]{1,0:T(8,128)(2,1)S(1)}, u32[]{:S(2)}, u32[]{:S(2)}) collective-permute-start(bf16[896,128]{1,0:T(8,128)(2,1)S(1)} %collective-permute-done.5), channel_id=1, source_target_pairs={{0,1},{1,0},{2,3},{3,2},{4,5},{5,4},{6,7},{7,6},{8,9},{9,8},{10,11... | collective-permute-start | bytes 688136 | tf_op jit(solution)/shard_map/ppermute | solution.py:321
